TPU v7x, 32 devices: a whole 2x2x4 slice. The times are simulated.
32 devices in a mesh: tm: 8 (over z, y), tensor: 4 (over x, core).
Axes of the slice: x: 2, y: 2, z: 4, core: 2. Of those that a mesh axis runs over, the one named last changes fastest.
Arguments:
- frames_in: bfloat16 [8, 528, 1024], P('tm'), may hold values from -6 to 6
- frame_time: int32 [8], replicated, may hold values from 0 to 7, each once
- cond_count: int32 [8], replicated, may hold values from 0 to 2
- ln1_gain: float32 [2, 1024], replicated, may hold values from 0.5 to 1.5
- ln1_bias: float32 [2, 1024], replicated, may hold values from -1.75 to 1.75
- qkv_weight: bfloat16 [2, 3, 1024, 1024], P(None, None, None, 'tensor'), may hold values from -17 to 17
- qkv_bias: float32 [2, 3, 1024], P(None, None, 'tensor'), may hold values from -1.75 to 1.75
- out_weight: bfloat16 [2, 1024, 1024], P(None, 'tensor'), may hold values from -0.1875 to 0.1875
- out_bias: float32 [2, 1024], replicated, may hold values from -1.75 to 1.75
- ln2_gain: float32 [2, 1024], replicated, may hold values from 0.5 to 1.5
- ln2_bias: float32 [2, 1024], replicated, may hold values from -1.75 to 1.75
- fc1_weight: bfloat16 [2, 1024, 4096], P(None, None, 'tensor'), may hold values from -0.1875 to 0.1875
- fc1_bias: float32 [2, 4096], P(None, 'tensor'), may hold values from -3 to 3
- fc2_weight: bfloat16 [2, 4096, 1024], P(None, 'tensor'), may hold values from -0.09375 to 0.09375
- fc2_bias: float32 [2, 1024], replicated, may hold values from -1.75 to 1.75
Outputs:
- frames_out: bfloat16 [8, 528, 1024], P('tm', 'tensor')
Inputs may be any that keep to these rules, and one draw needn't show every extreme that they name: `frame_time`: every time index 0 to 7 appears once. `cond_count`: the valid action and state tokens of a frame are its first ones.
All inputs are finite; a program needn't handle non-finite values.
Results may differ from a plain program's by a relative error of at most 0.04.
Values may be sent and summed in bfloat16 or wider, within the bound.
A program may use at most 128 MiB of HBM per device.

v0:
```python
import jax
import jax.numpy as jnp
from jax import lax
from jax.experimental import pallas as pl
from jax.experimental.pallas import tpu as pltpu
from jax.sharding import PartitionSpec as P

D = 1024
HEADS = 16
PATCH_DEV = 64
COND = 2
LAYERS = 2


def layer_norm(inputs, gain_row, bias_row):
    center = jnp.mean(inputs, axis=-1, keepdims=True)
    spread = jnp.mean(jnp.square(inputs - center), axis=-1, keepdims=True)
    return (inputs - center) * lax.rsqrt(spread + 1e-06) * gain_row + bias_row


def piece_tables(frame_time, cond_count, piece_count, frame_split, piece_rows):
    cond_dev = COND // frame_split
    piece_ids = jnp.arange(piece_count, dtype=jnp.int32)
    frame_ids = jnp.arange(frame_time.shape[0], dtype=jnp.int32)
    matches = (piece_ids // frame_split)[:, None] == frame_ids[None, :]
    piece_time = jnp.sum(jnp.where(matches, frame_time[None, :], 0), axis=1)
    piece_cond = jnp.sum(jnp.where(matches, cond_count[None, :], 0), axis=1)
    slot_index = jnp.arange(piece_rows, dtype=jnp.int32)
    cond_slot = (piece_ids % frame_split)[:, None] * cond_dev + slot_index[None, :] - PATCH_DEV
    valid = (slot_index[None, :] < PATCH_DEV) | (cond_slot < piece_cond[:, None])
    return (piece_time, valid)


def shards_gather(
    frames_in,
    frame_time,
    cond_count,
    ln1_gain,
    ln1_bias,
    qkv_weight,
    qkv_bias,
    out_weight,
    out_bias,
    ln2_gain,
    ln2_bias,
    fc1_weight,
    fc1_bias,
    fc2_weight,
    fc2_bias,
):
    frame_count = frame_time.shape[0]
    piece_count = lax.axis_size("tm")
    frame_split = piece_count // frame_count
    cond_dev = COND // frame_split
    piece_rows = PATCH_DEV + cond_dev
    row_count = frames_in.shape[1]
    seq_count = row_count // piece_rows
    head_dim = D // HEADS
    head_local = qkv_weight.shape[3] // head_dim
    scale = head_dim ** (-0.5)
    tensor_size = lax.axis_size("tensor")
    tensor_pos = lax.axis_index("tensor")
    my_piece = lax.axis_index("tm")
    share_rows = row_count // tensor_size
    piece_time, valid = piece_tables(frame_time, cond_count, piece_count, frame_split, piece_rows)
    piece_ids = jnp.arange(piece_count, dtype=jnp.int32)
    my_time = jnp.sum(jnp.where(piece_ids == my_piece, piece_time, 0))
    full_in = frames_in[0]
    new_share = None
    for layer_idx in range(LAYERS):
        normed = layer_norm(
            full_in.astype(jnp.float32), ln1_gain[layer_idx], ln1_bias[layer_idx]
        ).astype(jnp.bfloat16)
        projected = jnp.einsum(
            "rd,jde->jre", normed, qkv_weight[layer_idx], preferred_element_type=jnp.float32
        )
        projected = (projected + qkv_bias[layer_idx][:, None, :]).astype(jnp.bfloat16)
        queries = projected[0].reshape(seq_count, piece_rows, head_local, head_dim)
        keys_mine = projected[1].reshape(1, seq_count, piece_rows, head_local * head_dim)
        values_mine = projected[2].reshape(1, seq_count, piece_rows, head_local * head_dim)
        start_top = jnp.full((seq_count, head_local, piece_rows), -1e30, jnp.float32)
        key_block = lax.all_gather(keys_mine, "tm", axis=0, tiled=True)
        value_block = lax.all_gather(values_mine, "tm", axis=0, tiled=True)
        block_count = key_block.shape[0]
        block_ids = jnp.arange(block_count, dtype=jnp.int32)
        matches = block_ids[:, None] == piece_ids[None, :]
        key_time = jnp.sum(jnp.where(matches, piece_time[None, :], 0), axis=1)
        key_valid = jnp.any(matches[:, :, None] & valid[None, :, :], axis=1)
        allowed = (key_time <= my_time)[:, None] & key_valid
        top_run = start_top
        keys_split = key_block.reshape(block_count, seq_count, piece_rows, head_local, head_dim)
        values_split = value_block.reshape(block_count, seq_count, piece_rows, head_local, head_dim)
        scores = (
            jnp.einsum("sqhd,gskhd->shqgk", queries, keys_split, preferred_element_type=jnp.float32)
            * scale
        )
        scores = jnp.where(allowed, scores, -1e30)
        new_top = jnp.maximum(top_run, jnp.max(scores, axis=(3, 4)))
        weights = jnp.where(allowed, jnp.exp(scores - new_top[..., None, None]), 0.0)
        total_new = jnp.sum(weights, axis=(3, 4))
        mixed = jnp.einsum(
            "shqgk,gskhd->shqd",
            weights.astype(jnp.bfloat16),
            values_split,
            preferred_element_type=jnp.float32,
        )
        top_run = new_top
        attended = (
            (mixed / total_new[..., None])
            .transpose(0, 2, 1, 3)
            .reshape(row_count, head_local * head_dim)
            .astype(jnp.bfloat16)
        )
        out_layer = out_weight[layer_idx]
        fc1_layer = fc1_weight[layer_idx]
        fc2_layer = fc2_weight[layer_idx]
        fc1_layer_bias = fc1_bias[layer_idx]
        own_rows = lax.dynamic_slice_in_dim(full_in, tensor_pos * share_rows, share_rows, 0).astype(
            jnp.float32
        )
        first = (
            own_rows
            + lax.psum_scatter(
                jnp.dot(attended, out_layer, preferred_element_type=jnp.float32).astype(
                    jnp.bfloat16
                ),
                "tensor",
                scatter_dimension=0,
                tiled=True,
            ).astype(jnp.float32)
            + out_bias[layer_idx]
        )
        normed_two = layer_norm(first, ln2_gain[layer_idx], ln2_bias[layer_idx]).astype(
            jnp.bfloat16
        )
        inner = jax.nn.gelu(
            jnp.dot(
                lax.all_gather(normed_two, "tensor", axis=0, tiled=True),
                fc1_layer,
                preferred_element_type=jnp.float32,
            )
            + fc1_layer_bias,
            approximate=False,
        ).astype(jnp.bfloat16)
        mlp_share = lax.psum_scatter(
            jnp.dot(inner, fc2_layer, preferred_element_type=jnp.float32).astype(jnp.bfloat16),
            "tensor",
            scatter_dimension=0,
            tiled=True,
        ).astype(jnp.float32)
        new_share = (first + mlp_share + fc2_bias[layer_idx]).astype(jnp.bfloat16)
        if layer_idx + 1 < LAYERS:
            full_in = lax.all_gather(new_share, "tensor", axis=0, tiled=True)
    return new_share[None]


MESH = pl.DeviceIdType.MESH


def layers_kernel(
    share_ref, qt_ref, kt_ref, g1, b1, qkvb, ob, g2, b2, f1b, f2b, wqkv_h, wo_h, w1_h, w2_h,
    out_ref, wqkv, wo, w1, w2, ag1, ag2, qb, kb, vb, inner, xs, keep, keep_x, stage, rbuf,
    wsem, ssem, rsem,
):
    share = share_ref.shape[0]
    head_dim = D // HEADS
    width = qb.shape[1]
    head_local = width // head_dim
    me = lax.axis_index("tensor")
    partner = me + 1 - 2 * (me % 2)
    across = (me + 2) % 4
    diagonal = (partner + 2) % 4

    pairs = ((wqkv_h, wqkv), (wo_h, wo), (w1_h, w1), (w2_h, w2))

    def weight_copy(l, j):
        return pltpu.make_async_copy(pairs[j][0].at[l], pairs[j][1].at[l], wsem.at[l, j])

    for l in range(LAYERS):
        for j in range(4):
            weight_copy(l, j).start()

    barrier = pltpu.get_barrier_semaphore()
    for other in (partner, across, diagonal):
        pl.semaphore_signal(barrier, inc=1, device_id={"tensor": other}, device_id_type=MESH)
    pl.semaphore_wait(barrier, 3)

    def rows(s):
        return pl.ds(pl.multiple_of(s * share, 16), share)

    def send(src, dst, l, j, target):
        copy = pltpu.make_async_remote_copy(
            src_ref=src,
            dst_ref=dst,
            send_sem=ssem.at[l, j],
            recv_sem=rsem.at[l, j],
            device_id={"tensor": target},
            device_id_type=MESH,
        )
        copy.start()
        return copy

    def gather(buf, l, j, use):
        own = buf.at[l, rows(me)]
        to_x = send(own, own, l, j, across)
        to_p = send(own, own, l, j + 1, partner)
        use(0, me)
        to_p.wait_recv()
        use(1, partner)
        to_x.wait_recv()
        got = buf.at[l, rows(across)]
        fwd = send(got, got, l, j + 2, partner)
        use(2, across)
        fwd.wait_recv()
        use(3, diagonal)
        to_x.wait_send()
        to_p.wait_send()
        fwd.wait_send()

    def norm(x, gain, bias):
        return layer_norm(x, gain, bias).astype(jnp.bfloat16)

    lane = lax.broadcasted_iota(jnp.int32, (1, width), 1)

    def layer(l, carry):
        ag1[l, rows(me)] = norm(xs[...], g1[pl.ds(l, 1)], b1[pl.ds(l, 1)])
        weight_copy(l, 0).wait()

        def project(step, s):
            normed = ag1[l, rows(s)]
            for i, dst in enumerate((qb, kb, vb)):
                y = jnp.dot(normed, wqkv[l, i], preferred_element_type=jnp.float32) + qkvb[l, pl.ds(i, 1)]
                if i == 0:
                    y = y * head_dim ** (-0.5)
                dst[rows(s)] = y.astype(jnp.bfloat16)

        gather(ag1, l, 0, project)
        weight_copy(l, 1).wait()

        def attend(s):
            q = qb[rows(s)]
            allowed = kt_ref[...] <= qt_ref[rows(s)]
            acc = jnp.zeros((share, width), jnp.float32)
            for h in range(head_local):
                mine = (lane >= h * head_dim) & (lane < (h + 1) * head_dim)
                qm = q * jnp.where(mine, 1.0, 0.0).astype(jnp.bfloat16)
                sc = lax.dot_general(
                    qm, kb[...], (((1,), (1,)), ((), ())), preferred_element_type=jnp.float32
                )
                sc = jnp.where(allowed, sc, -1e30)
                w = jnp.exp(sc - jnp.max(sc, axis=-1, keepdims=True))
                total = jnp.sum(w, axis=-1, keepdims=True)
                pv = jnp.dot(w.astype(jnp.bfloat16), vb[...], preferred_element_type=jnp.float32)
                acc = jnp.where(mine, pv / total, acc)
            return jnp.dot(
                acc.astype(jnp.bfloat16), wo[l], preferred_element_type=jnp.float32
            )

        stage[0] = attend(diagonal).astype(jnp.bfloat16)
        c_f = send(stage.at[0], rbuf.at[l, 0], l, 3, partner)
        part = attend(across)
        c_f.wait_recv()
        stage[1] = (part + rbuf[l, 0].astype(jnp.float32)).astype(jnp.bfloat16)
        c_x = send(stage.at[1], rbuf.at[l, 1], l, 4, across)
        stage[2] = attend(partner).astype(jnp.bfloat16)
        c_p = send(stage.at[2], rbuf.at[l, 2], l, 5, partner)
        part = attend(me) + xs[...] + ob[pl.ds(l, 1)]
        c_p.wait_recv()
        part = part + rbuf[l, 2].astype(jnp.float32)
        c_x.wait_recv()
        first = part + rbuf[l, 1].astype(jnp.float32)
        xs[...] = first
        ag2[l, rows(me)] = norm(first, g2[pl.ds(l, 1)], b2[pl.ds(l, 1)])
        c_f.wait_send()
        c_x.wait_send()
        c_p.wait_send()
        weight_copy(l, 2).wait()
        weight_copy(l, 3).wait()

        def mlp(s):
            normed = ag2[l, rows(s)]
            tile = 256
            for n in range(w1.shape[2] // tile):
                at = pl.ds(n * tile, tile)
                y = jnp.dot(normed, w1[l, :, at], preferred_element_type=jnp.float32) + f1b[pl.ds(l, 1), at]
                y = 0.5 * y * (1.0 + lax.erf(y * (0.5**0.5)))
                inner[:, at] = y.astype(jnp.bfloat16)
            return jnp.dot(inner[...], w2[l], preferred_element_type=jnp.float32)

        copies = []

        def feed(step, s):
            part = mlp(s)
            if step == 0:
                keep[...] = part
            elif step == 1:
                stage[2] = part.astype(jnp.bfloat16)
                copies.append(send(stage.at[2], rbuf.at[l, 5], l, 11, partner))
            elif step == 2:
                keep_x[...] = part
            else:
                stage[0] = part.astype(jnp.bfloat16)
                copies.append(send(stage.at[0], rbuf.at[l, 3], l, 9, partner))

        gather(ag2, l, 6, feed)
        c_p, c_f = copies
        c_f.wait_recv()
        stage[1] = (keep_x[...] + rbuf[l, 3].astype(jnp.float32)).astype(jnp.bfloat16)
        c_x = send(stage.at[1], rbuf.at[l, 4], l, 10, across)
        c_p.wait_recv()
        part = keep[...] + xs[...] + f2b[pl.ds(l, 1)] + rbuf[l, 5].astype(jnp.float32)
        c_x.wait_recv()
        new = (part + rbuf[l, 4].astype(jnp.float32)).astype(jnp.bfloat16)
        xs[...] = new.astype(jnp.float32)
        c_p.wait_send()
        c_f.wait_send()
        c_x.wait_send()
        return carry

    xs[...] = share_ref[...].astype(jnp.float32)
    lax.fori_loop(0, LAYERS, layer, 0)
    out_ref[...] = xs[...].astype(jnp.bfloat16)


def swap_kernel(src_ref, dst_ref, ssem, rsem):
    count = src_ref.shape[0]
    tm, tensor = lax.axis_index("tm"), lax.axis_index("tensor")
    slot, column = tm % count, tm // count

    def away(j):
        return jnp.logical_or(tensor != column, slot != j)

    def remote(j):
        return pltpu.make_async_remote_copy(
            src_ref=src_ref.at[j],
            dst_ref=dst_ref.at[slot],
            send_sem=ssem.at[j],
            recv_sem=rsem.at[slot],
            device_id=(tensor * count + j, column),
            device_id_type=MESH,
        )

    def arrival(j):
        return pltpu.make_async_remote_copy(
            src_ref=src_ref.at[j],
            dst_ref=dst_ref.at[j],
            send_sem=ssem.at[j],
            recv_sem=rsem.at[j],
            device_id=(tensor * count + j, column),
            device_id_type=MESH,
        )

    def local(j):
        return pltpu.make_async_copy(src_ref.at[j], dst_ref.at[j], rsem.at[j])

    barrier = pltpu.get_barrier_semaphore()
    for j in range(count):

        @pl.when(away(j))
        def _():
            pl.semaphore_signal(
                barrier, inc=1, device_id=(tensor * count + j, column), device_id_type=MESH
            )

    @pl.when(tensor == column)
    def _():
        pl.semaphore_wait(barrier, count - 1)

    @pl.when(tensor != column)
    def _():
        pl.semaphore_wait(barrier, count)

    for j in range(count):

        @pl.when(away(j))
        def _():
            remote(j).start()

        @pl.when(jnp.logical_not(away(j)))
        def _():
            local(j).start()

    for j in range(count):

        @pl.when(away(j))
        def _():
            arrival(j).wait_recv()
            remote(j).wait_send()

        @pl.when(jnp.logical_not(away(j)))
        def _():
            local(j).wait()


def swap(blocks, collective_id):
    count = blocks.shape[0]
    return pl.pallas_call(
        swap_kernel,
        out_shape=jax.ShapeDtypeStruct(blocks.shape, blocks.dtype),
        in_specs=[pl.BlockSpec(memory_space=pltpu.VMEM)],
        out_specs=pl.BlockSpec(memory_space=pltpu.VMEM),
        scratch_shapes=[pltpu.SemaphoreType.DMA((count,)), pltpu.SemaphoreType.DMA((count,))],
        compiler_params=pltpu.CompilerParams(collective_id=collective_id, has_side_effects=True),
    )(blocks)


def shards_clip(
    frames_in,
    frame_time,
    cond_count,
    ln1_gain,
    ln1_bias,
    qkv_weight,
    qkv_bias,
    out_weight,
    out_bias,
    ln2_gain,
    ln2_bias,
    fc1_weight,
    fc1_bias,
    fc2_weight,
    fc2_bias,
):
    piece_count = lax.axis_size("tm")
    frame_split = piece_count // frame_time.shape[0]
    piece_rows = PATCH_DEV + COND // frame_split
    row_count = frames_in.shape[1]
    width = qkv_weight.shape[3]
    hidden = fc1_weight.shape[2]
    tensor_size = lax.axis_size("tensor")
    tensor_pos = lax.axis_index("tensor")
    share_rows = row_count // tensor_size
    share_pad = -(-share_rows // 16) * 16
    all_rows = share_pad * tensor_size
    piece_time, valid = piece_tables(frame_time, cond_count, piece_count, frame_split, piece_rows)
    far = jnp.int32(1 << 30)
    row_time = jnp.repeat(piece_time, piece_rows).reshape(tensor_size, share_rows)
    key_time = jnp.where(valid.reshape(tensor_size, share_rows), row_time, far)
    pad = ((0, 0), (0, share_pad - share_rows))
    row_time = jnp.pad(row_time, pad, constant_values=1 << 29).reshape(all_rows, 1)
    key_time = jnp.pad(key_time, pad, constant_values=1 << 30).reshape(1, all_rows)
    share = lax.dynamic_slice_in_dim(frames_in[0], tensor_pos * share_rows, share_rows, 0)
    share = swap(share.reshape(-1, piece_rows, D), 1).reshape(share_rows, D)
    share = jnp.pad(share, ((0, share_pad - share_rows), (0, 0)))

    vmem = pl.BlockSpec(memory_space=pltpu.VMEM)
    hbm = pl.BlockSpec(memory_space=pl.ANY)
    bf16, f32 = jnp.bfloat16, jnp.float32
    new_share = pl.pallas_call(
        layers_kernel,
        out_shape=jax.ShapeDtypeStruct((share_pad, D), bf16),
        in_specs=[vmem] * 11 + [hbm] * 4,
        out_specs=vmem,
        scratch_shapes=[
            pltpu.VMEM(qkv_weight.shape, bf16),
            pltpu.VMEM(out_weight.shape, bf16),
            pltpu.VMEM(fc1_weight.shape, bf16),
            pltpu.VMEM(fc2_weight.shape, bf16),
            pltpu.VMEM((LAYERS, all_rows, D), bf16),
            pltpu.VMEM((LAYERS, all_rows, D), bf16),
            pltpu.VMEM((all_rows, width), bf16),
            pltpu.VMEM((all_rows, width), bf16),
            pltpu.VMEM((all_rows, width), bf16),
            pltpu.VMEM((share_pad, hidden), bf16),
            pltpu.VMEM((share_pad, D), f32),
            pltpu.VMEM((share_pad, D), f32),
            pltpu.VMEM((share_pad, D), f32),
            pltpu.VMEM((3, share_pad, D), bf16),
            pltpu.VMEM((LAYERS, 6, share_pad, D), bf16),
            pltpu.SemaphoreType.DMA((LAYERS, 4)),
            pltpu.SemaphoreType.DMA((LAYERS, 12)),
            pltpu.SemaphoreType.DMA((LAYERS, 12)),
        ],
        compiler_params=pltpu.CompilerParams(
            collective_id=0, has_side_effects=True, vmem_limit_bytes=60 * 1024 * 1024
        ),
    )(
        share,
        row_time,
        key_time,
        ln1_gain,
        ln1_bias,
        qkv_bias,
        out_bias,
        ln2_gain,
        ln2_bias,
        fc1_bias,
        fc2_bias,
        qkv_weight,
        out_weight,
        fc1_weight,
        fc2_weight,
    )
    new_share = new_share[:share_rows].reshape(-1, piece_rows, D)
    return swap(new_share, 2).reshape(1, share_rows, D)


def shards(frames_in, frame_time, cond_count, *rest):
    frame_split = lax.axis_size("tm") // frame_time.shape[0]
    piece_rows = PATCH_DEV + COND // frame_split
    seq_count = frames_in.shape[1] // piece_rows
    by_clip = seq_count == lax.axis_size("tm") and lax.axis_size("tensor") == 4
    by_clip = by_clip and seq_count % 4 == 0
    body = shards_clip if by_clip else shards_gather
    return body(frames_in, frame_time, cond_count, *rest)


def solution(mesh):
    in_specs = (
        P("tm", None, None),
        P(),
        P(),
        P(),
        P(),
        P(None, None, None, "tensor"),
        P(None, None, "tensor"),
        P(None, "tensor", None),
        P(),
        P(),
        P(),
        P(None, None, "tensor"),
        P(None, "tensor"),
        P(None, "tensor", None),
        P(),
    )
    out_specs = P("tm", "tensor", None)
    return jax.shard_map(shards, mesh=mesh, in_specs=in_specs, out_specs=out_specs, check_vma=False)
```

profile of v0, /device:TPU:6, one launch (start us, length us, event | category | flops | bytes accessed | tf_op | source)
XLA Modules:
  0.0 136.8 jit_solution(13960278220705589910)
XLA Ops:
  0.0 0.0 copy-start
  0.0 0.9 select_reduce_fusion.1
  0.9 0.8 select_reduce_fusion
  1.7 0.1 or.14
  1.7 0.1 sub.9
  1.8 0.1 lt.34
  1.9 0.1 broadcast_in_dim.39
  2.0 0.1 broadcast_in_dim.40
  2.1 0.1 broadcast_in_dim.41
  2.2 0.1 lt.35
  2.2 0.1 lt.36
  2.3 0.7 reshape.46.kt_ref
  3.0 1.3 copy.20.qkvb
  4.3 0.0 copy-done
  4.3 0.1 constant_dynamic-slice_fusion
  4.4 0.8 reshape.43.src_ref
  5.2 20.1 %shard_map.145 = bf16[2,66,1024]{2,1,0:T(8,128)(2,1)} custom-call(bf16[2,66,1024]{2,1,0:T(8,128)(2,1)} %reshape.43.src_ref), custom_call_target="tpu_custom_call" | custom-call | tf_op jit(solution)/shard_map/pallas_call | solution.py:397
  25.3 1.0 reshape.44
  26.3 0.7 pad.11.share_ref
  27.1 0.9 reshape.49.qt_ref
  28.0 86.9 %shard_map.146 = bf16[144,1024]{1,0:T(8,128)(2,1)} custom-call(bf16[144,1024]{1,0:T(8,128)(2,1)} %pad.11.share_ref, s32[576,1]{1,0:T(8,128)} %reshape.49.qt_ref, s32[1,576]{1,0:T(1,128)} %reshape.46.kt_ref, f32[2,1024]{1,0:T(2,128)} %g1.1, f32[2,1024]{1,0:T(2,128)} %b1.1, f32[2,3,256]{2,1,0:T(4,128)} %copy.20.qkvb, f32[2,1024]{1,0:T(2,128)} %ob.1, ...), custom_call_target="tpu_custom_call" | custom-call | tf_op jit(solution)/shard_map/pallas_call | solution.py:449
  114.9 1.0 slice.3
  115.8 0.8 reshape.47.src_ref
  116.6 18.4 %shard_map.147 = bf16[2,66,1024]{2,1,0:T(8,128)(2,1)} custom-call(bf16[2,66,1024]{2,1,0:T(8,128)(2,1)} %reshape.47.src_ref), custom_call_target="tpu_custom_call" | custom-call | tf_op jit(solution)/shard_map/pallas_call | solution.py:397
  135.0 1.7 %reshape.48 = bf16[1,132,1024]{2,1,0:T(8,128)(2,1)} reshape(bf16[2,66,1024]{2,1,0:T(8,128)(2,1)} %shard_map.147) | data formatting | bytes 540672 | tf_op jit(solution)/shard_map/reshape | solution.py:495
  (6 shorter events, 0.0 us)
Async XLA Ops:
  0.0 4.3 %copy-start = (bf16[1,528,1024]{2,1,0:T(8,128)(2,1)S(1)}, bf16[1,528,1024]{2,1,0:T(8,128)(2,1)}, u32[]{:S(2)}) copy-start(bf16[1,528,1024]{2,1,0:T(8,128)(2,1)} %param.15) | copy-start | bytes 3244036
where the time goes:
time: 137 us
  Pallas kernels  125 us (91%)
  local copies, waits for them, and re-layouts  9.62 us (7%)
  other arithmetic  1.65 us (1%)
    pallas_call x1, Pallas kernels, shards_clip(): pl.pallas_call(layers_kernel, out_shape=jax.ShapeDtypeStruct((share_pad,...  86.9 us
    pallas_call x2, Pallas kernels, swap(): pl.pallas_call(swap_kernel, out_shape=jax.ShapeDtypeStruct(blocks.shape,...  38.6 us

commit v1 on v0

v1 whole, which is shorter than its diff:
```python
import jax
import jax.numpy as jnp
from jax import lax
from jax.experimental import pallas as pl
from jax.experimental.pallas import tpu as pltpu
from jax.sharding import PartitionSpec as P

D = 1024
HEADS = 16
PATCH_DEV = 64
COND = 2
LAYERS = 2


def layer_norm(inputs, gain_row, bias_row):
    center = jnp.mean(inputs, axis=-1, keepdims=True)
    spread = jnp.mean(jnp.square(inputs - center), axis=-1, keepdims=True)
    return (inputs - center) * lax.rsqrt(spread + 1e-06) * gain_row + bias_row


def piece_tables(frame_time, cond_count, piece_count, frame_split, piece_rows):
    cond_dev = COND // frame_split
    piece_ids = jnp.arange(piece_count, dtype=jnp.int32)
    frame_ids = jnp.arange(frame_time.shape[0], dtype=jnp.int32)
    matches = (piece_ids // frame_split)[:, None] == frame_ids[None, :]
    piece_time = jnp.sum(jnp.where(matches, frame_time[None, :], 0), axis=1)
    piece_cond = jnp.sum(jnp.where(matches, cond_count[None, :], 0), axis=1)
    slot_index = jnp.arange(piece_rows, dtype=jnp.int32)
    cond_slot = (piece_ids % frame_split)[:, None] * cond_dev + slot_index[None, :] - PATCH_DEV
    valid = (slot_index[None, :] < PATCH_DEV) | (cond_slot < piece_cond[:, None])
    return (piece_time, valid)


def shards_gather(
    frames_in,
    frame_time,
    cond_count,
    ln1_gain,
    ln1_bias,
    qkv_weight,
    qkv_bias,
    out_weight,
    out_bias,
    ln2_gain,
    ln2_bias,
    fc1_weight,
    fc1_bias,
    fc2_weight,
    fc2_bias,
):
    frame_count = frame_time.shape[0]
    piece_count = lax.axis_size("tm")
    frame_split = piece_count // frame_count
    cond_dev = COND // frame_split
    piece_rows = PATCH_DEV + cond_dev
    row_count = frames_in.shape[1]
    seq_count = row_count // piece_rows
    head_dim = D // HEADS
    head_local = qkv_weight.shape[3] // head_dim
    scale = head_dim ** (-0.5)
    tensor_size = lax.axis_size("tensor")
    tensor_pos = lax.axis_index("tensor")
    my_piece = lax.axis_index("tm")
    share_rows = row_count // tensor_size
    piece_time, valid = piece_tables(frame_time, cond_count, piece_count, frame_split, piece_rows)
    piece_ids = jnp.arange(piece_count, dtype=jnp.int32)
    my_time = jnp.sum(jnp.where(piece_ids == my_piece, piece_time, 0))
    full_in = frames_in[0]
    new_share = None
    for layer_idx in range(LAYERS):
        normed = layer_norm(
            full_in.astype(jnp.float32), ln1_gain[layer_idx], ln1_bias[layer_idx]
        ).astype(jnp.bfloat16)
        projected = jnp.einsum(
            "rd,jde->jre", normed, qkv_weight[layer_idx], preferred_element_type=jnp.float32
        )
        projected = (projected + qkv_bias[layer_idx][:, None, :]).astype(jnp.bfloat16)
        queries = projected[0].reshape(seq_count, piece_rows, head_local, head_dim)
        keys_mine = projected[1].reshape(1, seq_count, piece_rows, head_local * head_dim)
        values_mine = projected[2].reshape(1, seq_count, piece_rows, head_local * head_dim)
        start_top = jnp.full((seq_count, head_local, piece_rows), -1e30, jnp.float32)
        key_block = lax.all_gather(keys_mine, "tm", axis=0, tiled=True)
        value_block = lax.all_gather(values_mine, "tm", axis=0, tiled=True)
        block_count = key_block.shape[0]
        block_ids = jnp.arange(block_count, dtype=jnp.int32)
        matches = block_ids[:, None] == piece_ids[None, :]
        key_time = jnp.sum(jnp.where(matches, piece_time[None, :], 0), axis=1)
        key_valid = jnp.any(matches[:, :, None] & valid[None, :, :], axis=1)
        allowed = (key_time <= my_time)[:, None] & key_valid
        top_run = start_top
        keys_split = key_block.reshape(block_count, seq_count, piece_rows, head_local, head_dim)
        values_split = value_block.reshape(block_count, seq_count, piece_rows, head_local, head_dim)
        scores = (
            jnp.einsum("sqhd,gskhd->shqgk", queries, keys_split, preferred_element_type=jnp.float32)
            * scale
        )
        scores = jnp.where(allowed, scores, -1e30)
        new_top = jnp.maximum(top_run, jnp.max(scores, axis=(3, 4)))
        weights = jnp.where(allowed, jnp.exp(scores - new_top[..., None, None]), 0.0)
        total_new = jnp.sum(weights, axis=(3, 4))
        mixed = jnp.einsum(
            "shqgk,gskhd->shqd",
            weights.astype(jnp.bfloat16),
            values_split,
            preferred_element_type=jnp.float32,
        )
        top_run = new_top
        attended = (
            (mixed / total_new[..., None])
            .transpose(0, 2, 1, 3)
            .reshape(row_count, head_local * head_dim)
            .astype(jnp.bfloat16)
        )
        out_layer = out_weight[layer_idx]
        fc1_layer = fc1_weight[layer_idx]
        fc2_layer = fc2_weight[layer_idx]
        fc1_layer_bias = fc1_bias[layer_idx]
        own_rows = lax.dynamic_slice_in_dim(full_in, tensor_pos * share_rows, share_rows, 0).astype(
            jnp.float32
        )
        first = (
            own_rows
            + lax.psum_scatter(
                jnp.dot(attended, out_layer, preferred_element_type=jnp.float32).astype(
                    jnp.bfloat16
                ),
                "tensor",
                scatter_dimension=0,
                tiled=True,
            ).astype(jnp.float32)
            + out_bias[layer_idx]
        )
        normed_two = layer_norm(first, ln2_gain[layer_idx], ln2_bias[layer_idx]).astype(
            jnp.bfloat16
        )
        inner = jax.nn.gelu(
            jnp.dot(
                lax.all_gather(normed_two, "tensor", axis=0, tiled=True),
                fc1_layer,
                preferred_element_type=jnp.float32,
            )
            + fc1_layer_bias,
            approximate=False,
        ).astype(jnp.bfloat16)
        mlp_share = lax.psum_scatter(
            jnp.dot(inner, fc2_layer, preferred_element_type=jnp.float32).astype(jnp.bfloat16),
            "tensor",
            scatter_dimension=0,
            tiled=True,
        ).astype(jnp.float32)
        new_share = (first + mlp_share + fc2_bias[layer_idx]).astype(jnp.bfloat16)
        if layer_idx + 1 < LAYERS:
            full_in = lax.all_gather(new_share, "tensor", axis=0, tiled=True)
    return new_share[None]


MESH = pl.DeviceIdType.MESH
FAR = 1 << 30
N1, AP, AD, AO, N2, RP, XS = 0, 2, 4, 6, 8, 10, 12
IDS = 14
OWN, PIECE, REST, SPREAD = 0, 1, 2, 3


def clip_kernel(
    x_ref, time_ref, cond_ref, g1, b1, qkvb, ob, g2, b2, f1b, f2b, wqkv_h, wo_h, w1_h, w2_h,
    out_ref, wqkv, wo, w1, w2, blk_s, blk_r, xs, keep, nrm1, nrm2, qb, kb, vb, mask, att, att_p,
    inner, stg, rp, us, ur, out_s, out_r,
    wsem, in_s, in_r, fw_s, fw_r, loc, ls, lr, ws, wr, os, orr,
):
    groups = blk_s.shape[0]
    half = blk_r.shape[0]
    piece = blk_r.shape[1]
    patch = PATCH_DEV
    rows = xs.shape[0]
    lead = rows - half * patch
    cut = lead + (half // 2) * patch
    chunks = ((0, cut), (cut, rows - cut))
    head_dim = D // HEADS
    width = qb.shape[1]
    head_local = width // head_dim
    share = width // groups
    last = LAYERS - 1

    t = lax.axis_index("tm")
    me = lax.axis_index("tensor")
    x = me // 2
    c = me % 2
    partner = me + 1 - 2 * c
    across = (me + 2) % 4
    diagonal = (partner + 2) % 4

    def clip_of(g):
        return g // 2 + half * ((g // 2 + g) % 2)

    def group_of(clip):
        z = clip % half
        return 2 * z + (clip // half + z) % 2

    clip = clip_of(t)
    goal_x = clip // half
    goal = clip // 2

    pairs = ((wqkv_h, wqkv), (wo_h, wo), (w1_h, w1), (w2_h, w2))

    def weight_copy(l, j):
        dst = pairs[j][1].at[l]
        if j == 1:
            dst = wo.at[l, pl.ds(pl.multiple_of(me * width, width), width)]
        return pltpu.make_async_copy(pairs[j][0].at[l], dst, wsem.at[l, j])

    for l in range(LAYERS):
        for j in ((1, 0, 2, 3) if l == 0 else (0, 1, 2, 3)):
            weight_copy(l, j).start()

    def remote(src, dst, s, r, to):
        return pltpu.make_async_remote_copy(
            src_ref=src, dst_ref=dst, send_sem=s, recv_sem=r, device_id=to, device_id_type=MESH
        )

    barrier = pltpu.get_barrier_semaphore()

    def hello(g, j):
        pl.semaphore_signal(barrier, inc=1, device_id=(g, j), device_id_type=MESH)

    for other in (partner, across, diagonal):
        hello(t, other)
    for d in range(1, groups):
        hello((t + d) % groups, me)
    for s in range(2):
        g = group_of(2 * me + s)
        j = x * 2 + t // half

        @pl.when(jnp.logical_or(g != t, j != me))
        def _():
            hello(g, j)

    for g in range(groups):
        blk_s[g] = x_ref[g * piece : (g + 1) * piece]

    home = c == t // half
    own_copy = pltpu.make_async_copy(blk_s.at[clip], blk_r.at[t % half], loc.at[0])

    @pl.when(home)
    def _():
        own_copy.start()

    def times(axis, query):
        shape = (2 * rows, 1) if axis == 0 else (1, 2 * rows)
        at = lax.broadcasted_iota(jnp.int32, shape, axis)
        out = jnp.full(shape, FAR // 2 if query else FAR, jnp.int32)
        for f in range(groups):
            base = (f // half) * rows
            lo = base + lead + (f % half) * patch
            out = jnp.where((at >= lo) & (at < lo + patch), time_ref[f], out)
            lo = base + COND * (f % half)
            hi = lo + (COND if query else cond_ref[f])
            out = jnp.where((at >= lo) & (at < hi), time_ref[f], out)
        return out

    mask[...] = jnp.where(times(1, False) <= times(0, True), 0.0, -1e30)
    xs[0:lead] = jnp.zeros((lead, D), jnp.float32)

    targets = jnp.where(x == goal_x, half, 0)
    targets = targets - jnp.where((x == goal_x) & (goal == me) & home, 1, 0)
    pl.semaphore_wait(barrier, 3 + groups - 1 + targets)

    def enter(i):
        g = 2 * i + (t + x) % 2
        return g, remote(
            blk_s.at[clip_of(g)], blk_r.at[t % half], in_s.at[i], in_r.at[t % half], (g, me)
        )

    for i in range(half):
        g, copy = enter(i)

        @pl.when(home & (g != t))
        def _():
            copy.start()

    def span(j, first, count):
        return pl.ds(pl.multiple_of(j * width + first, share), count)

    def wo_own(l):
        at = wo.at[l, span(me, 0, width)]
        return remote(at, at, ws.at[l, OWN], wr.at[l, OWN], (t, partner))

    def wo_piece(l):
        at = wo.at[l, span(me, share * t, share)]
        return remote(at, at, ws.at[l, PIECE], wr.at[l, PIECE], (t, across))

    def wo_spread(l, d):
        at = wo.at[l, span(across, share * t, share)]
        return remote(
            at, at, ws.at[l, SPREAD + d], wr.at[l, SPREAD + d], ((t + d) % groups, me)
        )

    def wo_rest(l):
        at = wo.at[l, span(across, 0, width)]
        return remote(at, at, ws.at[l, REST], wr.at[l, REST], (t, partner))

    def wo_begin(l):
        weight_copy(l, 1).wait()
        wo_own(l).start()
        wo_piece(l).start()

    def wo_share(l):
        wo_piece(l).wait_recv()
        for d in range(1, groups):
            wo_spread(l, d).start()

    def wo_finish(l):
        for d in range(1, groups):
            wo_spread(l, d).wait_recv()
        wo_rest(l).start()

    def onward(k):
        return remote(blk_r.at[k], blk_r.at[k], fw_s.at[k], fw_r.at[k], (t, across))

    def arrival(k):
        return remote(blk_s.at[0], blk_r.at[k], in_s.at[0], in_r.at[k], (t, across))

    base = (x + t) % 2
    for i in range(half // 2):
        k = base + 2 * i
        mine = half * c + k == t

        @pl.when(jnp.logical_not(mine))
        def _():
            arrival(k).wait_recv()
            onward(k).start()

    wo_begin(0)
    wo_share(0)

    for i in range(half // 2):
        k = 1 - base + 2 * i
        mine = half * c + k == t

        @pl.when(jnp.logical_not(mine))
        def _():
            onward(k).wait_recv()

    @pl.when(home)
    def _():
        own_copy.wait()

    for k in range(half):
        block = blk_r[k].astype(jnp.float32)
        xs[lead + k * patch : lead + (k + 1) * patch] = block[:patch]
        xs[COND * k : COND * (k + 1)] = block[patch:]

    def norm(v, gain, bias):
        return layer_norm(v, gain, bias).astype(jnp.bfloat16)

    def in_half(h, r0, count):
        return pl.ds(pl.multiple_of(h * rows + r0, 16), count)

    def send1(l, i):
        r0, m = chunks[i]
        at = nrm1.at[l, c, pl.ds(r0, m)]
        return remote(at, at, ls.at[l, N1 + i], lr.at[l, N1 + i], (t, partner))

    def send2(l, i):
        r0, m = chunks[i]
        at = nrm2.at[l, c, pl.ds(r0, m)]
        return remote(at, at, ls.at[l, N2 + i], lr.at[l, N2 + i], (t, partner))

    def come1(l, i):
        r0, m = chunks[i]
        at = nrm1.at[l, 1 - c, pl.ds(r0, m)]
        return remote(at, at, ls.at[l, N1 + i], lr.at[l, N1 + i], (t, partner))

    def come2(l, i):
        r0, m = chunks[i]
        at = nrm2.at[l, 1 - c, pl.ds(r0, m)]
        return remote(at, at, ls.at[l, N2 + i], lr.at[l, N2 + i], (t, partner))

    def att_send(l, i, kind):
        r0, m = chunks[i]
        to = {AP: partner, AD: diagonal, AO: across}[kind]
        src = att.at[l, me, pl.ds(r0, m)] if kind == AO else att_p.at[l, pl.ds(r0, m)]
        return remote(
            src, att.at[l, me, pl.ds(r0, m)], ls.at[l, kind + i], lr.at[l, kind + i], (t, to)
        )

    def att_come(l, i, kind):
        r0, m = chunks[i]
        at = {AP: partner, AD: diagonal, AO: across}[kind]
        dst = att.at[l, at, pl.ds(r0, m)]
        return remote(dst, dst, ls.at[l, kind + i], lr.at[l, kind + i], (t, at))

    def sum_send(l, i):
        r0, m = chunks[i]
        at = pl.ds(r0, m)
        return remote(
            stg.at[l, at], rp.at[l, at], ls.at[l, RP + i], lr.at[l, RP + i], (t, partner)
        )

    def cross_send(l, i):
        r0, m = chunks[i]
        at = pl.ds(r0, m)
        return remote(us.at[l, at], ur.at[l, at], ls.at[l, XS + i], lr.at[l, XS + i], (t, across))

    def leave(k):
        return remote(
            out_s.at[k], out_r.at[clip % 2], os.at[k], orr.at[clip % 2], (half * c + k, goal)
        )

    def stay(k):
        return pltpu.make_async_copy(out_s.at[k], out_r.at[clip % 2], orr.at[clip % 2])

    for i, (r0, m) in enumerate(chunks):
        nrm1[0, c, r0 : r0 + m] = norm(xs[r0 : r0 + m], g1[0:1], b1[0:1])
        send1(0, i).start()

    lane = lax.broadcasted_iota(jnp.int32, (1, width), 1)
    heads = [(lane >= h * head_dim) & (lane < (h + 1) * head_dim) for h in range(head_local)]

    def layer(l, carry):
        weight_copy(l, 0).wait()

        def project(h, i):
            r0, m = chunks[i]
            normed = nrm1[l, h, r0 : r0 + m]
            for j, dst in enumerate((qb, kb, vb)):
                y = jnp.dot(normed, wqkv[l, j], preferred_element_type=jnp.float32)
                y = y + qkvb[j, pl.ds(l, 1)]
                if j == 0:
                    y = y * head_dim ** (-0.5)
                dst[in_half(h, r0, m)] = y.astype(jnp.bfloat16)

        for i in range(2):
            project(c, i)
        for i in range(2):
            come1(l, i).wait_recv()
            project(1 - c, i)

        def attend(h, i):
            r0, m = chunks[i]
            q = qb[in_half(h, r0, m)]
            stacked = jnp.concatenate(
                [q * jnp.where(on, 1.0, 0.0).astype(jnp.bfloat16) for on in heads], axis=0
            )
            sc = lax.dot_general(
                stacked, kb[...], (((1,), (1,)), ((), ())), preferred_element_type=jnp.float32
            )
            hide = mask[in_half(h, r0, m)]
            parts, totals = [], []
            for j in range(head_local):
                s = sc[j * m : (j + 1) * m] + hide
                w = jnp.exp(s - jnp.max(s, axis=-1, keepdims=True))
                totals.append(jnp.sum(w, axis=-1, keepdims=True))
                parts.append(w.astype(jnp.bfloat16))
            pv = jnp.dot(
                jnp.concatenate(parts, axis=0), vb[...], preferred_element_type=jnp.float32
            )
            acc = jnp.zeros((m, width), jnp.float32)
            for j in range(head_local):
                acc = jnp.where(heads[j], pv[j * m : (j + 1) * m] * (1.0 / totals[j]), acc)
            return acc.astype(jnp.bfloat16)

        for i, (r0, m) in enumerate(chunks):
            att_p[l, r0 : r0 + m] = attend(1 - c, i)
            att_send(l, i, AD).start()
            att_send(l, i, AP).start()
            att[l, me, r0 : r0 + m] = attend(c, i)
            att_send(l, i, AO).start()
            if i == 0:
                wo_finish(l)

        @pl.when(l < last)
        def _():
            wo_begin(l + 1)
            wo_share(l + 1)

        wo_own(l).wait_recv()
        wo_rest(l).wait_recv()
        for i, (r0, m) in enumerate(chunks):
            for kind in (AP, AD, AO):
                att_come(l, i, kind).wait_recv()
            full = jnp.concatenate([att[l, j, r0 : r0 + m] for j in range(4)], axis=1)
            first = jnp.dot(full, wo[l], preferred_element_type=jnp.float32)
            first = xs[r0 : r0 + m] + first + ob[pl.ds(l, 1)]
            xs[r0 : r0 + m] = first
            nrm2[l, c, r0 : r0 + m] = norm(first, g2[pl.ds(l, 1)], b2[pl.ds(l, 1)])
            send2(l, i).start()

        weight_copy(l, 2).wait()
        weight_copy(l, 3).wait()

        def mlp(h, i):
            r0, m = chunks[i]
            normed = nrm2[l, h, r0 : r0 + m]
            tile = 256
            for n in range(w1.shape[2] // tile):
                at = pl.ds(n * tile, tile)
                y = jnp.dot(normed, w1[l, :, at], preferred_element_type=jnp.float32)
                y = y + f1b[pl.ds(l, 1), at]
                y = 0.5 * y * (1.0 + lax.erf(y * (0.5**0.5)))
                inner[0:m, at] = y.astype(jnp.bfloat16)
            return jnp.dot(inner[0:m], w2[l], preferred_element_type=jnp.float32)

        sends_x = jnp.logical_or(l < last, x != goal_x)
        takes_x = jnp.logical_or(l < last, x == goal_x)

        def combine(i):
            r0, m = chunks[i]
            sum_send(l, i).wait_recv()
            u = keep[r0 : r0 + m] + rp[l, r0 : r0 + m].astype(jnp.float32)
            keep[r0 : r0 + m] = u
            us[l, r0 : r0 + m] = u.astype(jnp.bfloat16)

            @pl.when(sends_x)
            def _():
                cross_send(l, i).start()

        for i, (r0, m) in enumerate(chunks):
            keep[r0 : r0 + m] = mlp(c, i)
            if i > 0:
                combine(i - 1)
            come2(l, i).wait_recv()
            stg[l, r0 : r0 + m] = mlp(1 - c, i).astype(jnp.bfloat16)
            sum_send(l, i).start()
        combine(1)

        for i, (r0, m) in enumerate(chunks):

            @pl.when(takes_x)
            def _():
                cross_send(l, i).wait_recv()
                new = xs[r0 : r0 + m] + keep[r0 : r0 + m] + f2b[pl.ds(l, 1)]
                new = (new + ur[l, r0 : r0 + m].astype(jnp.float32)).astype(jnp.bfloat16)

                @pl.when(l < last)
                def _():
                    wide = new.astype(jnp.float32)
                    xs[r0 : r0 + m] = wide
                    nrm1[l + 1, c, r0 : r0 + m] = norm(
                        wide, g1[pl.ds(l + 1, 1)], b1[pl.ds(l + 1, 1)]
                    )
                    send1(l + 1, i).start()

                @pl.when(l == last)
                def _():
                    if i == 0:
                        for k in range(half):
                            out_s[k, patch:piece] = new[COND * k : COND * (k + 1)]
                    skip = lead if i == 0 else 0
                    for k in range(half // 2):
                        block = new[skip + k * patch : skip + (k + 1) * patch]
                        out_s[k + i * (half // 2), 0:patch] = block
                    for k in range(i * (half // 2), (i + 1) * (half // 2)):
                        here = (half * c + k == t) & (goal == me)

                        @pl.when(here)
                        def _():
                            stay(k).start()

                        @pl.when(jnp.logical_not(here))
                        def _():
                            leave(k).start()

        for i in range(2):
            send1(l, i).wait_send()
            send2(l, i).wait_send()
            for kind in (AP, AD, AO):
                att_send(l, i, kind).wait_send()
            sum_send(l, i).wait_send()

            @pl.when(sends_x)
            def _():
                cross_send(l, i).wait_send()

        wo_own(l).wait_send()
        wo_piece(l).wait_send()
        wo_rest(l).wait_send()
        for d in range(1, groups):
            wo_spread(l, d).wait_send()
        return carry

    lax.fori_loop(0, LAYERS, layer, 0)

    for i in range(half):
        g, copy = enter(i)

        @pl.when(home & (g != t))
        def _():
            copy.wait_send()

    for i in range(half // 2):
        k = base + 2 * i

        @pl.when(half * c + k != t)
        def _():
            onward(k).wait_send()

    for s in range(2):
        there = 2 * me + s
        here = (group_of(there) == t) & (x * 2 + t // half == me)

        @pl.when(here)
        def _():
            pltpu.make_async_copy(out_s.at[t % half], out_r.at[s], orr.at[s]).wait()

        @pl.when(jnp.logical_not(here))
        def _():
            remote(out_s.at[0], out_r.at[s], os.at[0], orr.at[s], (t, across)).wait_recv()

        out_ref[s * piece : (s + 1) * piece] = out_r[s]

    for k in range(half):
        here = (half * c + k == t) & (goal == me)

        @pl.when((x == goal_x) & jnp.logical_not(here))
        def _():
            leave(k).wait_send()


def shards_clip(
    frames_in,
    frame_time,
    cond_count,
    ln1_gain,
    ln1_bias,
    qkv_weight,
    qkv_bias,
    out_weight,
    out_bias,
    ln2_gain,
    ln2_bias,
    fc1_weight,
    fc1_bias,
    fc2_weight,
    fc2_bias,
):
    groups = lax.axis_size("tm")
    tensor_size = lax.axis_size("tensor")
    piece = PATCH_DEV + COND
    half = groups // 2
    width = qkv_weight.shape[3]
    hidden = fc1_weight.shape[2]
    lead = -(-half * COND // 16) * 16
    rows = lead + half * PATCH_DEV
    cut = lead + (half // 2) * PATCH_DEV

    vmem = pl.BlockSpec(memory_space=pltpu.VMEM)
    smem = pl.BlockSpec(memory_space=pltpu.SMEM)
    hbm = pl.BlockSpec(memory_space=pl.ANY)
    bf16, f32 = jnp.bfloat16, jnp.float32
    dma = pltpu.SemaphoreType.DMA
    out = pl.pallas_call(
        clip_kernel,
        out_shape=jax.ShapeDtypeStruct((2 * piece, D), bf16),
        in_specs=[vmem, smem, smem] + [vmem] * 8 + [hbm] * 4,
        out_specs=vmem,
        scratch_shapes=[
            pltpu.VMEM(qkv_weight.shape, bf16),
            pltpu.VMEM((LAYERS, D, D), bf16),
            pltpu.VMEM(fc1_weight.shape, bf16),
            pltpu.VMEM(fc2_weight.shape, bf16),
            pltpu.VMEM((groups, piece, D), bf16),
            pltpu.VMEM((half, piece, D), bf16),
            pltpu.VMEM((rows, D), f32),
            pltpu.VMEM((rows, D), f32),
            pltpu.VMEM((LAYERS, 2, rows, D), bf16),
            pltpu.VMEM((LAYERS, 2, rows, D), bf16),
            pltpu.VMEM((2 * rows, width), bf16),
            pltpu.VMEM((2 * rows, width), bf16),
            pltpu.VMEM((2 * rows, width), bf16),
            pltpu.VMEM((2 * rows, 2 * rows), f32),
            pltpu.VMEM((LAYERS, tensor_size, rows, width), bf16),
            pltpu.VMEM((LAYERS, rows, width), bf16),
            pltpu.VMEM((cut, hidden), bf16),
            pltpu.VMEM((LAYERS, rows, D), bf16),
            pltpu.VMEM((LAYERS, rows, D), bf16),
            pltpu.VMEM((LAYERS, rows, D), bf16),
            pltpu.VMEM((LAYERS, rows, D), bf16),
            pltpu.VMEM((half, piece, D), bf16),
            pltpu.VMEM((2, piece, D), bf16),
            dma((LAYERS, 4)),
            dma((half,)),
            dma((half,)),
            dma((half,)),
            dma((half,)),
            dma((1,)),
            dma((LAYERS, IDS)),
            dma((LAYERS, IDS)),
            dma((LAYERS, SPREAD + groups)),
            dma((LAYERS, SPREAD + groups)),
            dma((half,)),
            dma((2,)),
        ],
        compiler_params=pltpu.CompilerParams(
            collective_id=0, has_side_effects=True, vmem_limit_bytes=60 * 1024 * 1024
        ),
    )(
        frames_in[0],
        frame_time,
        cond_count,
        ln1_gain,
        ln1_bias,
        qkv_bias.transpose(1, 0, 2),
        out_bias,
        ln2_gain,
        ln2_bias,
        fc1_bias,
        fc2_bias,
        qkv_weight,
        out_weight,
        fc1_weight,
        fc2_weight,
    )
    return out[None]


def shards(frames_in, frame_time, cond_count, *rest):
    groups = lax.axis_size("tm")
    seq_count = frames_in.shape[1] // (PATCH_DEV + COND)
    by_clip = frame_time.shape[0] == groups and seq_count == groups
    by_clip = by_clip and lax.axis_size("tensor") == 4 and groups == 8
    body = shards_clip if by_clip else shards_gather
    return body(frames_in, frame_time, cond_count, *rest)


def solution(mesh):
    in_specs = (
        P("tm", None, None),
        P(),
        P(),
        P(),
        P(),
        P(None, None, None, "tensor"),
        P(None, None, "tensor"),
        P(None, "tensor", None),
        P(),
        P(),
        P(),
        P(None, None, "tensor"),
        P(None, "tensor"),
        P(None, "tensor", None),
        P(),
    )
    out_specs = P("tm", "tensor", None)
    return jax.shard_map(shards, mesh=mesh, in_specs=in_specs, out_specs=out_specs, check_vma=False)
```

time: 137 us -> 99.7 us (0.73)
  the two profiles are of different devices: /device:TPU:6 before, /device:TPU:13 now
where the time goes in v1:
time: 99.7 us; the launch traced here: 99.5 us
  Pallas kernels  97.8 us (98%)
  local copies, waits for them, and re-layouts  1.68 us (2%)
    pallas_call x1, Pallas kernels, shards_clip(): pl.pallas_call(clip_kernel, out_shape=jax.ShapeDtypeStruct((2 * piece, D)...  97.8 us

profile of v1, /device:TPU:13, one launch (start us, length us, event | category | flops | bytes accessed | tf_op | source)
XLA Modules:
  0.0 99.5 jit_solution(4069090948065428633)
XLA Ops:
  0.0 97.8 %shard_map.145 = bf16[132,1024]{1,0:T(8,128)(2,1)} custom-call(bf16[528,1024]{1,0:T(8,128)(2,1)} %bitcast.4, s32[8]{0:T(128)} %time_ref.1, s32[8]{0:T(128)} %cond_ref.1, f32[2,1024]{1,0:T(2,128)} %g1.1, f32[2,1024]{1,0:T(2,128)} %b1.1, f32[3,2,256]{2,1,0:T(2,128)} %bitcast.5, f32[2,1024]{1,0:T(2,128)} %ob.1, f32[2,1024]{1,0:T(2,128)} %g2.1, f32[2,1024]{1,0:T(2,128)} %b2.1, ...), custom_call_target="tpu_custom_call" | custom-call | tf_op jit(solution)/shard_map/pallas_call | solution.py:651
  97.8 1.7 %copy.17 = bf16[1,132,1024]{2,1,0:T(8,128)(2,1)} copy(bf16[1,132,1024]{2,1,0:T(8,128)(2,1)} %bitcast.3) | data formatting | bytes 540672

commit v2 on v1

--- a/solution.py
+++ b/solution.py
@@ -156,16 +156,15 @@
 
 MESH = pl.DeviceIdType.MESH
 FAR = 1 << 30
-N1, AP, AD, AO, N2, RP, XS = 0, 2, 4, 6, 8, 10, 12
-IDS = 14
-OWN, PIECE, REST, SPREAD = 0, 1, 2, 3
+N1, AP, AD, AO, XS = range(5)
+OWN, PIECE, REST, UP, DOWN, SPREAD = range(6)
 
 
 def clip_kernel(
     x_ref, time_ref, cond_ref, g1, b1, qkvb, ob, g2, b2, f1b, f2b, wqkv_h, wo_h, w1_h, w2_h,
-    out_ref, wqkv, wo, w1, w2, blk_s, blk_r, xs, keep, nrm1, nrm2, qb, kb, vb, mask, att, att_p,
-    inner, stg, rp, us, ur, out_s, out_r,
-    wsem, in_s, in_r, fw_s, fw_r, loc, ls, lr, ws, wr, os, orr,
+    out_ref, wqkv, wo, w1, w2, w1p, w2p, f1p, blk_s, blk_r, xs, keep, nrm1, nrm2, qb, kb, vb, mask,
+    att, att_p, inner, us, ur, out_s, out_r,
+    wsem, in_s, in_r, fw_s, fw_r, loc, bs, br, ls, lr, ws, wr, os, orr,
 ):
     groups = blk_s.shape[0]
     half = blk_r.shape[0]
@@ -173,8 +172,11 @@
     patch = PATCH_DEV
     rows = xs.shape[0]
     lead = rows - half * patch
+    chunks = [(lead + i * patch, patch) for i in range(half)]
+    chunks[0] = (0, lead + patch)
     cut = lead + (half // 2) * patch
-    chunks = ((0, cut), (cut, rows - cut))
+    spans = ((0, cut), (cut, rows - cut))
+    per = half // 2
     head_dim = D // HEADS
     width = qb.shape[1]
     head_local = width // head_dim
@@ -186,6 +188,7 @@
     x = me // 2
     c = me % 2
     partner = me + 1 - 2 * c
+    beside = t + 1 - 2 * (t % 2)
     across = (me + 2) % 4
     diagonal = (partner + 2) % 4
 
@@ -262,10 +265,13 @@
 
     targets = jnp.where(x == goal_x, half, 0)
     targets = targets - jnp.where((x == goal_x) & (goal == me) & home, 1, 0)
-    pl.semaphore_wait(barrier, 3 + groups - 1 + targets)
+    with jax.named_scope("barrier"):
+        pl.semaphore_wait(barrier, 3 + groups - 1 + targets)
 
     def enter(i):
-        g = 2 * i + (t + x) % 2
+        far = jnp.where(x == 0, t // 2 + 2, half - 1 - t // 2)
+        z = (far + 2 * (i // 2)) % half
+        g = 2 * z + i % 2
         return g, remote(
             blk_s.at[clip_of(g)], blk_r.at[t % half], in_s.at[i], in_r.at[t % half], (g, me)
         )
@@ -288,30 +294,56 @@
         at = wo.at[l, span(me, share * t, share)]
         return remote(at, at, ws.at[l, PIECE], wr.at[l, PIECE], (t, across))
 
-    def wo_spread(l, d):
-        at = wo.at[l, span(across, share * t, share)]
-        return remote(
-            at, at, ws.at[l, SPREAD + d], wr.at[l, SPREAD + d], ((t + d) % groups, me)
-        )
+    def wo_slice(l, g):
+        return wo.at[l, span(across, share * g, share)]
+
+    def wo_column(l, d, g):
+        at = wo_slice(l, g)
+        to = (t + 2 * d) % groups
+        return remote(at, at, ws.at[l, SPREAD + d], wr.at[l, SPREAD + d], (to, me))
+
+    def wo_row(l, d, g):
+        at = wo_slice(l, g)
+        j = SPREAD + half + d
+        return remote(at, at, ws.at[l, j], wr.at[l, j], (beside, me))
 
     def wo_rest(l):
         at = wo.at[l, span(across, 0, width)]
         return remote(at, at, ws.at[l, REST], wr.at[l, REST], (t, partner))
 
+    def mlp_weights(l):
+        return [
+            remote(src.at[l], dst.at[l], ws.at[l, j], wr.at[l, j], (t, partner))
+            for j, src, dst in ((UP, w1_h, w1p), (DOWN, w2_h, w2p))
+        ]
+
     def wo_begin(l):
         weight_copy(l, 1).wait()
+        wo_piece(l).start()
         wo_own(l).start()
-        wo_piece(l).start()
 
     def wo_share(l):
         wo_piece(l).wait_recv()
-        for d in range(1, groups):
-            wo_spread(l, d).start()
+        for d in range(1, half):
+            wo_column(l, d, t).start()
+        wo_row(l, 0, t).start()
+
+    def wo_relay(l):
+        for d in range(1, half):
+            g = (t - 2 * d + groups) % groups
+            wo_column(l, d, g).wait_recv()
+            wo_row(l, d, g).start()
 
     def wo_finish(l):
-        for d in range(1, groups):
-            wo_spread(l, d).wait_recv()
+        for d in range(half):
+            wo_row(l, d, (beside - 2 * d + groups) % groups).wait_recv()
         wo_rest(l).start()
+
+    bias_copy = remote(f1b, f1p, bs.at[0], br.at[0], (t, partner))
+    wo_begin(0)
+    bias_copy.start()
+    for copy in mlp_weights(0):
+        copy.start()
 
     def onward(k):
         return remote(blk_r.at[k], blk_r.at[k], fw_s.at[k], fw_r.at[k], (t, across))
@@ -319,35 +351,18 @@
     def arrival(k):
         return remote(blk_s.at[0], blk_r.at[k], in_s.at[0], in_r.at[k], (t, across))
 
-    base = (x + t) % 2
-    for i in range(half // 2):
-        k = base + 2 * i
-        mine = half * c + k == t
-
-        @pl.when(jnp.logical_not(mine))
-        def _():
-            arrival(k).wait_recv()
+    first_k = per * ((t // 2 + x) % 2)
+    with jax.named_scope("wo_first"):
+        wo_share(0)
+
+    for i in range(per):
+        k = first_k + i
+
+        @pl.when(half * c + k != t)
+        def _():
+            with jax.named_scope("in_direct"):
+                arrival(k).wait_recv()
             onward(k).start()
-
-    wo_begin(0)
-    wo_share(0)
-
-    for i in range(half // 2):
-        k = 1 - base + 2 * i
-        mine = half * c + k == t
-
-        @pl.when(jnp.logical_not(mine))
-        def _():
-            onward(k).wait_recv()
-
-    @pl.when(home)
-    def _():
-        own_copy.wait()
-
-    for k in range(half):
-        block = blk_r[k].astype(jnp.float32)
-        xs[lead + k * patch : lead + (k + 1) * patch] = block[:patch]
-        xs[COND * k : COND * (k + 1)] = block[patch:]
 
     def norm(v, gain, bias):
         return layer_norm(v, gain, bias).astype(jnp.bfloat16)
@@ -355,51 +370,31 @@
     def in_half(h, r0, count):
         return pl.ds(pl.multiple_of(h * rows + r0, 16), count)
 
-    def send1(l, i):
-        r0, m = chunks[i]
-        at = nrm1.at[l, c, pl.ds(r0, m)]
-        return remote(at, at, ls.at[l, N1 + i], lr.at[l, N1 + i], (t, partner))
-
-    def send2(l, i):
-        r0, m = chunks[i]
-        at = nrm2.at[l, c, pl.ds(r0, m)]
-        return remote(at, at, ls.at[l, N2 + i], lr.at[l, N2 + i], (t, partner))
-
-    def come1(l, i):
-        r0, m = chunks[i]
-        at = nrm1.at[l, 1 - c, pl.ds(r0, m)]
-        return remote(at, at, ls.at[l, N1 + i], lr.at[l, N1 + i], (t, partner))
-
-    def come2(l, i):
-        r0, m = chunks[i]
-        at = nrm2.at[l, 1 - c, pl.ds(r0, m)]
-        return remote(at, at, ls.at[l, N2 + i], lr.at[l, N2 + i], (t, partner))
+    def ids(l, kind, i):
+        return ls.at[l, kind * (half + 1) + i], lr.at[l, kind * (half + 1) + i]
+
+    def normed_send(l, i):
+        at = nrm1.at[l, c, pl.ds(*chunks[i])]
+        return remote(at, at, *ids(l, N1, i), (t, partner))
+
+    def normed_come(l, i):
+        at = nrm1.at[l, 1 - c, pl.ds(*chunks[i])]
+        return remote(at, at, *ids(l, N1, i), (t, partner))
 
     def att_send(l, i, kind):
-        r0, m = chunks[i]
+        at = pl.ds(*spans[i])
         to = {AP: partner, AD: diagonal, AO: across}[kind]
-        src = att.at[l, me, pl.ds(r0, m)] if kind == AO else att_p.at[l, pl.ds(r0, m)]
-        return remote(
-            src, att.at[l, me, pl.ds(r0, m)], ls.at[l, kind + i], lr.at[l, kind + i], (t, to)
-        )
+        src = att.at[l, me, at] if kind == AO else att_p.at[l, at]
+        return remote(src, att.at[l, me, at], *ids(l, kind, i), (t, to))
 
     def att_come(l, i, kind):
-        r0, m = chunks[i]
-        at = {AP: partner, AD: diagonal, AO: across}[kind]
-        dst = att.at[l, at, pl.ds(r0, m)]
-        return remote(dst, dst, ls.at[l, kind + i], lr.at[l, kind + i], (t, at))
-
-    def sum_send(l, i):
-        r0, m = chunks[i]
-        at = pl.ds(r0, m)
-        return remote(
-            stg.at[l, at], rp.at[l, at], ls.at[l, RP + i], lr.at[l, RP + i], (t, partner)
-        )
+        to = {AP: partner, AD: diagonal, AO: across}[kind]
+        dst = att.at[l, to, pl.ds(*spans[i])]
+        return remote(dst, dst, *ids(l, kind, i), (t, to))
 
     def cross_send(l, i):
-        r0, m = chunks[i]
-        at = pl.ds(r0, m)
-        return remote(us.at[l, at], ur.at[l, at], ls.at[l, XS + i], lr.at[l, XS + i], (t, across))
+        at = pl.ds(*chunks[i])
+        return remote(us.at[l, at], ur.at[l, at], *ids(l, XS, i), (t, across))
 
     def leave(k):
         return remote(
@@ -409,34 +404,79 @@
     def stay(k):
         return pltpu.make_async_copy(out_s.at[k], out_r.at[clip % 2], orr.at[clip % 2])
 
-    for i, (r0, m) in enumerate(chunks):
-        nrm1[0, c, r0 : r0 + m] = norm(xs[r0 : r0 + m], g1[0:1], b1[0:1])
-        send1(0, i).start()
+    def project(l, h, r0, m):
+        at = pl.ds(r0 if isinstance(r0, int) else pl.multiple_of(r0, 16), m)
+        normed = nrm1[l, h, at]
+        for j, dst in enumerate((qb, kb, vb)):
+            y = jnp.dot(normed, wqkv[l, j], preferred_element_type=jnp.float32)
+            y = y + qkvb[j, pl.ds(l, 1)]
+            if j == 0:
+                y = y * head_dim ** (-0.5)
+            dst[in_half(h, r0, m)] = y.astype(jnp.bfloat16)
+
+    def strip(i):
+        return pl.ds(pl.multiple_of(lead + i * patch, 16), patch) if i is not None else pl.ds(0, lead)
+
+    def block_send(h, i):
+        at = nrm1.at[0, h, strip(i)]
+        return remote(at, at, *ids(0, N1, half if i is None else i), (t, partner))
+
+    def normed_in(i):
+        at = strip(i)
+        nrm1[0, c, at] = norm(xs[at], g1[0:1], b1[0:1])
+        block_send(c, i).start()
+
+    def take(k):
+        xs[strip(k)] = blk_r[k, 0:patch].astype(jnp.float32)
+        normed_in(k)
+        project(0, c, lead + k * patch, patch)
+
+    def take_other(k):
+        with jax.named_scope("n1_wait"):
+            block_send(1 - c, k).wait_recv()
+        project(0, 1 - c, lead + k * patch, patch)
+
+    weight_copy(0, 0).wait()
+    for i in range(per):
+        k = first_k + i
+
+        @pl.when(half * c + k == t)
+        def _():
+            own_copy.wait()
+
+        take(k)
+    with jax.named_scope("wo_relay"):
+        wo_relay(0)
+    for i in range(per):
+        k = per - first_k + i
+
+        @pl.when(half * c + k == t)
+        def _():
+            own_copy.wait()
+
+        @pl.when(half * c + k != t)
+        def _():
+            with jax.named_scope("in_cross"):
+                onward(k).wait_recv()
+
+        take(k)
+        take_other(first_k + i)
+    for k in range(half):
+        xs[COND * k : COND * (k + 1)] = blk_r[k, patch:piece].astype(jnp.float32)
+    normed_in(None)
+    for l in range(1, LAYERS):
+        wo_begin(l)
+    project(0, c, 0, lead)
+    for i in range(per):
+        take_other(per - first_k + i)
+    block_send(1 - c, None).wait_recv()
+    project(0, 1 - c, 0, lead)
 
     lane = lax.broadcasted_iota(jnp.int32, (1, width), 1)
     heads = [(lane >= h * head_dim) & (lane < (h + 1) * head_dim) for h in range(head_local)]
 
     def layer(l, carry):
-        weight_copy(l, 0).wait()
-
-        def project(h, i):
-            r0, m = chunks[i]
-            normed = nrm1[l, h, r0 : r0 + m]
-            for j, dst in enumerate((qb, kb, vb)):
-                y = jnp.dot(normed, wqkv[l, j], preferred_element_type=jnp.float32)
-                y = y + qkvb[j, pl.ds(l, 1)]
-                if j == 0:
-                    y = y * head_dim ** (-0.5)
-                dst[in_half(h, r0, m)] = y.astype(jnp.bfloat16)
-
-        for i in range(2):
-            project(c, i)
-        for i in range(2):
-            come1(l, i).wait_recv()
-            project(1 - c, i)
-
-        def attend(h, i):
-            r0, m = chunks[i]
+        def attend(h, r0, m):
             q = qb[in_half(h, r0, m)]
             stacked = jnp.concatenate(
                 [q * jnp.where(on, 1.0, 0.0).astype(jnp.bfloat16) for on in heads], axis=0
@@ -459,75 +499,100 @@
                 acc = jnp.where(heads[j], pv[j * m : (j + 1) * m] * (1.0 / totals[j]), acc)
             return acc.astype(jnp.bfloat16)
 
-        for i, (r0, m) in enumerate(chunks):
-            att_p[l, r0 : r0 + m] = attend(1 - c, i)
+        for i, (r0, m) in enumerate(spans):
+            with jax.named_scope("attend_other"):
+                att_p[l, r0 : r0 + m] = attend(1 - c, r0, m)
             att_send(l, i, AD).start()
             att_send(l, i, AP).start()
-            att[l, me, r0 : r0 + m] = attend(c, i)
+            with jax.named_scope("attend_own"):
+                att[l, me, r0 : r0 + m] = attend(c, r0, m)
             att_send(l, i, AO).start()
             if i == 0:
-                wo_finish(l)
+                with jax.named_scope("wo_finish"):
+                    wo_finish(l)
 
         @pl.when(l < last)
         def _():
-            wo_begin(l + 1)
-            wo_share(l + 1)
-
-        wo_own(l).wait_recv()
-        wo_rest(l).wait_recv()
-        for i, (r0, m) in enumerate(chunks):
-            for kind in (AP, AD, AO):
-                att_come(l, i, kind).wait_recv()
+            for copy in mlp_weights(l + 1):
+                copy.start()
+
+        with jax.named_scope("wo_rest_wait"):
+            wo_own(l).wait_recv()
+            wo_rest(l).wait_recv()
+        weight_copy(l, 2).wait()
+        weight_copy(l, 3).wait()
+
+        def ready(i, r0, m):
+            with jax.named_scope("att_wait"):
+                for kind in (AP, AD, AO):
+                    att_come(l, i, kind).wait_recv()
             full = jnp.concatenate([att[l, j, r0 : r0 + m] for j in range(4)], axis=1)
             first = jnp.dot(full, wo[l], preferred_element_type=jnp.float32)
             first = xs[r0 : r0 + m] + first + ob[pl.ds(l, 1)]
             xs[r0 : r0 + m] = first
-            nrm2[l, c, r0 : r0 + m] = norm(first, g2[pl.ds(l, 1)], b2[pl.ds(l, 1)])
-            send2(l, i).start()
-
-        weight_copy(l, 2).wait()
-        weight_copy(l, 3).wait()
-
-        def mlp(h, i):
-            r0, m = chunks[i]
-            normed = nrm2[l, h, r0 : r0 + m]
+            nrm2[0:m] = norm(first, g2[pl.ds(l, 1)], b2[pl.ds(l, 1)])
+
+        def mlp(m):
             tile = 256
-            for n in range(w1.shape[2] // tile):
-                at = pl.ds(n * tile, tile)
-                y = jnp.dot(normed, w1[l, :, at], preferred_element_type=jnp.float32)
-                y = y + f1b[pl.ds(l, 1), at]
-                y = 0.5 * y * (1.0 + lax.erf(y * (0.5**0.5)))
-                inner[0:m, at] = y.astype(jnp.bfloat16)
-            return jnp.dot(inner[0:m], w2[l], preferred_element_type=jnp.float32)
+            hidden = w1.shape[2]
+            total = 0.0
+            for p, (up, bias, down) in enumerate(((w1, f1b, w2), (w1p, f1p, w2p))):
+                for n in range(hidden // tile):
+                    at = pl.ds(n * tile, tile)
+                    y = jnp.dot(nrm2[0:m], up[l, :, at], preferred_element_type=jnp.float32)
+                    y = y + bias[pl.ds(l, 1), at]
+                    y = 0.5 * y * (1.0 + lax.erf(y * (0.5**0.5)))
+                    inner[0:m, pl.ds(n * tile, tile)] = y.astype(jnp.bfloat16)
+                total = total + jnp.dot(
+                    inner[0:m], down[l], preferred_element_type=jnp.float32
+                )
+            return total
 
         sends_x = jnp.logical_or(l < last, x != goal_x)
         takes_x = jnp.logical_or(l < last, x == goal_x)
 
-        def combine(i):
-            r0, m = chunks[i]
-            sum_send(l, i).wait_recv()
-            u = keep[r0 : r0 + m] + rp[l, r0 : r0 + m].astype(jnp.float32)
-            keep[r0 : r0 + m] = u
-            us[l, r0 : r0 + m] = u.astype(jnp.bfloat16)
+        for i, (r0, m) in enumerate(spans):
+            ready(i, r0, m)
+            if i == 0:
+                with jax.named_scope("weights_wait"):
+
+                    @pl.when(l == 0)
+                    def _():
+                        bias_copy.wait_recv()
+
+                    for copy in mlp_weights(l):
+                        copy.wait_recv()
+            with jax.named_scope("mlp"):
+                u = mlp(m)
+                keep[r0 : r0 + m] = u
+                us[l, r0 : r0 + m] = u.astype(jnp.bfloat16)
 
             @pl.when(sends_x)
             def _():
-                cross_send(l, i).start()
-
-        for i, (r0, m) in enumerate(chunks):
-            keep[r0 : r0 + m] = mlp(c, i)
-            if i > 0:
-                combine(i - 1)
-            come2(l, i).wait_recv()
-            stg[l, r0 : r0 + m] = mlp(1 - c, i).astype(jnp.bfloat16)
-            sum_send(l, i).start()
-        combine(1)
+                for j in range(per * i, per * (i + 1)):
+                    cross_send(l, j).start()
+
+            if i == 0:
+
+                @pl.when(l < last)
+                def _():
+                    wo_share(l + 1)
+
+        @pl.when(l < last)
+        def _():
+            weight_copy(l + 1, 0).wait()
+
+        def other(i):
+            with jax.named_scope("n1_wait"):
+                normed_come(l + 1, i).wait_recv()
+            project(l + 1, 1 - c, *chunks[i])
 
         for i, (r0, m) in enumerate(chunks):
 
             @pl.when(takes_x)
             def _():
-                cross_send(l, i).wait_recv()
+                with jax.named_scope("x_wait"):
+                    cross_send(l, i).wait_recv()
                 new = xs[r0 : r0 + m] + keep[r0 : r0 + m] + f2b[pl.ds(l, 1)]
                 new = (new + ur[l, r0 : r0 + m].astype(jnp.float32)).astype(jnp.bfloat16)
 
@@ -538,82 +603,111 @@
                     nrm1[l + 1, c, r0 : r0 + m] = norm(
                         wide, g1[pl.ds(l + 1, 1)], b1[pl.ds(l + 1, 1)]
                     )
-                    send1(l + 1, i).start()
+                    normed_send(l + 1, i).start()
+                    project(l + 1, c, r0, m)
+                    if i > 0:
+                        other(i - 1)
 
                 @pl.when(l == last)
                 def _():
                     if i == 0:
                         for k in range(half):
                             out_s[k, patch:piece] = new[COND * k : COND * (k + 1)]
-                    skip = lead if i == 0 else 0
-                    for k in range(half // 2):
-                        block = new[skip + k * patch : skip + (k + 1) * patch]
-                        out_s[k + i * (half // 2), 0:patch] = block
-                    for k in range(i * (half // 2), (i + 1) * (half // 2)):
-                        here = (half * c + k == t) & (goal == me)
-
-                        @pl.when(here)
-                        def _():
-                            stay(k).start()
-
-                        @pl.when(jnp.logical_not(here))
-                        def _():
-                            leave(k).start()
-
-        for i in range(2):
-            send1(l, i).wait_send()
-            send2(l, i).wait_send()
+                    out_s[i, 0:patch] = new[m - patch :]
+                    here = (half * c + i == t) & (goal == me)
+
+                    @pl.when(here)
+                    def _():
+                        stay(i).start()
+
+                    @pl.when(jnp.logical_not(here))
+                    def _():
+                        leave(i).start()
+
+            if i == half - 3:
+
+                @pl.when(l < last)
+                def _():
+                    with jax.named_scope("wo_relay"):
+                        wo_relay(l + 1)
+
+        @pl.when(l < last)
+        def _():
+            other(half - 1)
+
+        return carry
+
+    lax.fori_loop(0, LAYERS, layer, 0)
+
+    for i in range(half):
+        g, copy = enter(i)
+
+        @pl.when(home & (g != t))
+        def _():
+            copy.wait_send()
+
+    for i in range(per):
+        k = first_k + i
+
+        @pl.when(half * c + k != t)
+        def _():
+            onward(k).wait_send()
+
+    for s in range(2):
+        there = 2 * me + s
+        here = (group_of(there) == t) & (x * 2 + t // half == me)
+
+        @pl.when(here)
+        def _():
+            pltpu.make_async_copy(out_s.at[t % half], out_r.at[s], orr.at[s]).wait()
+
+        @pl.when(jnp.logical_not(here))
+        def _():
+            with jax.named_scope("out_wait"):
+                remote(out_s.at[0], out_r.at[s], os.at[0], orr.at[s], (t, across)).wait_recv()
+
+        out_ref[s * piece : (s + 1) * piece] = out_r[s]
+
+    for k in range(half):
+        here = (half * c + k == t) & (goal == me)
+
+        @pl.when((x == goal_x) & jnp.logical_not(here))
+        def _():
+            leave(k).wait_send()
+
+    bias_copy.wait_send()
+
+    for i in range(half):
+        block_send(c, i).wait_send()
+    block_send(c, None).wait_send()
+
+    def drain(l, carry):
+        for i in range(half):
+
+            @pl.when(l > 0)
+            def _():
+                normed_send(l, i).wait_send()
+
+            @pl.when(jnp.logical_or(l < last, x != goal_x))
+            def _():
+                cross_send(l, i).wait_send()
+
+        for i in range(len(spans)):
             for kind in (AP, AD, AO):
                 att_send(l, i, kind).wait_send()
-            sum_send(l, i).wait_send()
-
-            @pl.when(sends_x)
-            def _():
-                cross_send(l, i).wait_send()
 
         wo_own(l).wait_send()
         wo_piece(l).wait_send()
         wo_rest(l).wait_send()
-        for d in range(1, groups):
-            wo_spread(l, d).wait_send()
+        for d in range(1, half):
+            wo_column(l, d, t).wait_send()
+        for d in range(half):
+            wo_row(l, d, t).wait_send()
+        for copy in mlp_weights(l):
+            copy.wait_send()
         return carry
 
-    lax.fori_loop(0, LAYERS, layer, 0)
-
-    for i in range(half):
-        g, copy = enter(i)
-
-        @pl.when(home & (g != t))
-        def _():
-            copy.wait_send()
-
-    for i in range(half // 2):
-        k = base + 2 * i
-
-        @pl.when(half * c + k != t)
-        def _():
-            onward(k).wait_send()
-
-    for s in range(2):
-        there = 2 * me + s
-        here = (group_of(there) == t) & (x * 2 + t // half == me)
-
-        @pl.when(here)
-        def _():
-            pltpu.make_async_copy(out_s.at[t % half], out_r.at[s], orr.at[s]).wait()
-
-        @pl.when(jnp.logical_not(here))
-        def _():
-            remote(out_s.at[0], out_r.at[s], os.at[0], orr.at[s], (t, across)).wait_recv()
-
-        out_ref[s * piece : (s + 1) * piece] = out_r[s]
-
-    for k in range(half):
-        here = (half * c + k == t) & (goal == me)
-
-        @pl.when((x == goal_x) & jnp.logical_not(here))
-        def _():
-            leave(k).wait_send()
+    lax.fori_loop(0, LAYERS, drain, 0)
 
 
 def shards_clip(
@@ -641,7 +735,7 @@
     hidden = fc1_weight.shape[2]
     lead = -(-half * COND // 16) * 16
     rows = lead + half * PATCH_DEV
-    cut = lead + (half // 2) * PATCH_DEV
+    chunk = lead + (half // 2) * PATCH_DEV
 
     vmem = pl.BlockSpec(memory_space=pltpu.VMEM)
     smem = pl.BlockSpec(memory_space=pltpu.SMEM)
@@ -658,21 +752,22 @@
             pltpu.VMEM((LAYERS, D, D), bf16),
             pltpu.VMEM(fc1_weight.shape, bf16),
             pltpu.VMEM(fc2_weight.shape, bf16),
+            pltpu.VMEM(fc1_weight.shape, bf16),
+            pltpu.VMEM(fc2_weight.shape, bf16),
+            pltpu.VMEM(fc1_bias.shape, f32),
             pltpu.VMEM((groups, piece, D), bf16),
             pltpu.VMEM((half, piece, D), bf16),
             pltpu.VMEM((rows, D), f32),
             pltpu.VMEM((rows, D), f32),
             pltpu.VMEM((LAYERS, 2, rows, D), bf16),
-            pltpu.VMEM((LAYERS, 2, rows, D), bf16),
+            pltpu.VMEM((chunk, D), bf16),
             pltpu.VMEM((2 * rows, width), bf16),
             pltpu.VMEM((2 * rows, width), bf16),
             pltpu.VMEM((2 * rows, width), bf16),
             pltpu.VMEM((2 * rows, 2 * rows), f32),
             pltpu.VMEM((LAYERS, tensor_size, rows, width), bf16),
             pltpu.VMEM((LAYERS, rows, width), bf16),
-            pltpu.VMEM((cut, hidden), bf16),
-            pltpu.VMEM((LAYERS, rows, D), bf16),
-            pltpu.VMEM((LAYERS, rows, D), bf16),
+            pltpu.VMEM((chunk, hidden), bf16),
             pltpu.VMEM((LAYERS, rows, D), bf16),
             pltpu.VMEM((LAYERS, rows, D), bf16),
             pltpu.VMEM((half, piece, D), bf16),
@@ -683,10 +778,12 @@
             dma((half,)),
             dma((half,)),
             dma((1,)),
-            dma((LAYERS, IDS)),
-            dma((LAYERS, IDS)),
-            dma((LAYERS, SPREAD + groups)),
-            dma((LAYERS, SPREAD + groups)),
+            dma((1,)),
+            dma((1,)),
+            dma((LAYERS, 5 * (half + 1))),
+            dma((LAYERS, 5 * (half + 1))),
+            dma((LAYERS, SPREAD + 2 * half)),
+            dma((LAYERS, SPREAD + 2 * half)),
             dma((half,)),
             dma((2,)),
         ],

time: 99.7 us -> 82.7 us (0.83)
  the two profiles are of different devices: /device:TPU:13 before, /device:TPU:0 now
where the time goes in v2:
time: 82.7 us; the launch traced here: 81.7 us
  Pallas kernels  80 us (97%)
  local copies, waits for them, and re-layouts  1.68 us (2%)
    pallas_call x1, Pallas kernels, shards_clip(): pl.pallas_call(clip_kernel, out_shape=jax.ShapeDtypeStruct((2 * piece, D)...  80 us
    unnamed x1, local copies, waits for them, and re-layouts  1.68 us

profile of v2, /device:TPU:0, one launch (start us, length us, event | category | flops | bytes accessed | tf_op | source)
XLA Modules:
  0.0 81.7 jit_solution(11990873603496420425)
XLA Ops:
  0.0 80.0 %shard_map.145 = bf16[132,1024]{1,0:T(8,128)(2,1)} custom-call(bf16[528,1024]{1,0:T(8,128)(2,1)} %bitcast.4, s32[8]{0:T(128)} %time_ref.1, s32[8]{0:T(128)} %cond_ref.1, f32[2,1024]{1,0:T(2,128)} %g1.1, f32[2,1024]{1,0:T(2,128)} %b1.1, f32[3,2,256]{2,1,0:T(2,128)} %bitcast.5, f32[2,1024]{1,0:T(2,128)} %ob.1, f32[2,1024]{1,0:T(2,128)} %g2.1, f32[2,1024]{1,0:T(2,128)} %b2.1, ...), custom_call_target="tpu_custom_call" | custom-call | tf_op jit(solution)/shard_map/pallas_call | solution.py:745
  80.0 1.7 %copy.17 = bf16[1,132,1024]{2,1,0:T(8,128)(2,1)} copy(bf16[1,132,1024]{2,1,0:T(8,128)(2,1)} %bitcast.3) | data formatting | bytes 540672

commit v3 on v2

--- a/solution.py
+++ b/solution.py
@@ -162,14 +162,14 @@
 
 def clip_kernel(
     x_ref, time_ref, cond_ref, g1, b1, qkvb, ob, g2, b2, f1b, f2b, wqkv_h, wo_h, w1_h, w2_h,
-    out_ref, wqkv, wo, w1, w2, w1p, w2p, f1p, blk_s, blk_r, xs, keep, nrm1, nrm2, qb, kb, vb, mask,
-    att, att_p, inner, us, ur, out_s, out_r,
+    out_ref, wqkv, wo, w1, w2, w1p, w2p, f1p, blk_s, cnd_s, blk_r, cnd_r, xs, keep, nrm1, nrm2, qb, kb, vb, mask,
+    att, att_p, inner, us, ur, out_s, out_r, ocn_s, ocn_r,
     wsem, in_s, in_r, fw_s, fw_r, loc, bs, br, ls, lr, ws, wr, os, orr,
 ):
     groups = blk_s.shape[0]
     half = blk_r.shape[0]
-    piece = blk_r.shape[1]
     patch = PATCH_DEV
+    piece = patch + COND
     rows = xs.shape[0]
     lead = rows - half * patch
     chunks = [(lead + i * patch, patch) for i in range(half)]
@@ -238,14 +238,19 @@
             hello(g, j)
 
     for g in range(groups):
-        blk_s[g] = x_ref[g * piece : (g + 1) * piece]
+        blk_s[g] = x_ref[g * piece : g * piece + patch]
+        cnd_s[g] = x_ref[g * piece + patch : (g + 1) * piece]
 
     home = c == t // half
-    own_copy = pltpu.make_async_copy(blk_s.at[clip], blk_r.at[t % half], loc.at[0])
+    own_copies = [
+        pltpu.make_async_copy(src.at[clip], dst.at[t % half], loc.at[j])
+        for j, (src, dst) in enumerate(((blk_s, blk_r), (cnd_s, cnd_r)))
+    ]
 
     @pl.when(home)
     def _():
-        own_copy.start()
+        for copy in own_copies:
+            copy.start()
 
     def times(axis, query):
         shape = (2 * rows, 1) if axis == 0 else (1, 2 * rows)
@@ -268,20 +273,21 @@
     with jax.named_scope("barrier"):
         pl.semaphore_wait(barrier, 3 + groups - 1 + targets)
 
-    def enter(i):
+    def enter(i, j):
         far = jnp.where(x == 0, t // 2 + 2, half - 1 - t // 2)
         z = (far + 2 * (i // 2)) % half
-        g = 2 * z + i % 2
-        return g, remote(
-            blk_s.at[clip_of(g)], blk_r.at[t % half], in_s.at[i], in_r.at[t % half], (g, me)
-        )
-
-    for i in range(half):
-        g, copy = enter(i)
-
-        @pl.when(home & (g != t))
-        def _():
-            copy.start()
+        g = 2 * z + (i + t) % 2
+        k = t % half
+        src, dst = ((blk_s, blk_r), (cnd_s, cnd_r))[j]
+        return g, remote(src.at[clip_of(g)], dst.at[k], in_s.at[j, i], in_r.at[j, k], (g, me))
+
+    for j in range(2):
+        for i in range(half):
+            g, copy = enter(i, j)
+
+            @pl.when(home & (g != t))
+            def _():
+                copy.start()
 
     def span(j, first, count):
         return pl.ds(pl.multiple_of(j * width + first, share), count)
@@ -328,11 +334,10 @@
             wo_column(l, d, t).start()
         wo_row(l, 0, t).start()
 
-    def wo_relay(l):
-        for d in range(1, half):
-            g = (t - 2 * d + groups) % groups
-            wo_column(l, d, g).wait_recv()
-            wo_row(l, d, g).start()
+    def wo_relay(l, d):
+        g = (t - 2 * d + groups) % groups
+        wo_column(l, d, g).wait_recv()
+        wo_row(l, d, g).start()
 
     def wo_finish(l):
         for d in range(half):
@@ -345,18 +350,26 @@
     for copy in mlp_weights(0):
         copy.start()
 
-    def onward(k):
-        return remote(blk_r.at[k], blk_r.at[k], fw_s.at[k], fw_r.at[k], (t, across))
-
-    def arrival(k):
-        return remote(blk_s.at[0], blk_r.at[k], in_s.at[0], in_r.at[k], (t, across))
+    def onward(k, j=0):
+        at = (blk_r, cnd_r)[j].at[k]
+        return remote(at, at, fw_s.at[j, k], fw_r.at[j, k], (t, across))
+
+    def arrival(k, j=0):
+        src, dst = ((blk_s, blk_r), (cnd_s, cnd_r))[j]
+        return remote(src.at[0], dst.at[k], in_s.at[j, 0], in_r.at[j, k], (t, across))
 
     first_k = per * ((t // 2 + x) % 2)
     with jax.named_scope("wo_first"):
         wo_share(0)
 
+    def near(i):
+        return first_k + (i + t) % 2
+
+    def cross(i):
+        return per - first_k + (i + t) % 2
+
     for i in range(per):
-        k = first_k + i
+        k = near(i)
 
         @pl.when(half * c + k != t)
         def _():
@@ -396,13 +409,25 @@
         at = pl.ds(*chunks[i])
         return remote(us.at[l, at], ur.at[l, at], *ids(l, XS, i), (t, across))
 
-    def leave(k):
-        return remote(
-            out_s.at[k], out_r.at[clip % 2], os.at[k], orr.at[clip % 2], (half * c + k, goal)
-        )
-
-    def stay(k):
-        return pltpu.make_async_copy(out_s.at[k], out_r.at[clip % 2], orr.at[clip % 2])
+    def leave(k, j=0):
+        src, dst = ((out_s, out_r), (ocn_s, ocn_r))[j]
+        s = clip % 2
+        return remote(src.at[k], dst.at[s], os.at[j, k], orr.at[j, s], (half * c + k, goal))
+
+    def stay(k, j=0):
+        src, dst = ((out_s, out_r), (ocn_s, ocn_r))[j]
+        return pltpu.make_async_copy(src.at[k], dst.at[clip % 2], orr.at[j, clip % 2])
+
+    def depart(k, j=0):
+        here = (half * c + k == t) & (goal == me)
+
+        @pl.when(here)
+        def _():
+            stay(k, j).start()
+
+        @pl.when(jnp.logical_not(here))
+        def _():
+            leave(k, j).start()
 
     def project(l, h, r0, m):
         at = pl.ds(r0 if isinstance(r0, int) else pl.multiple_of(r0, 16), m)
@@ -427,7 +452,7 @@
         block_send(c, i).start()
 
     def take(k):
-        xs[strip(k)] = blk_r[k, 0:patch].astype(jnp.float32)
+        xs[strip(k)] = blk_r[k].astype(jnp.float32)
         normed_in(k)
         project(0, c, lead + k * patch, patch)
 
@@ -436,23 +461,23 @@
             block_send(1 - c, k).wait_recv()
         project(0, 1 - c, lead + k * patch, patch)
 
+    def local(k):
+        @pl.when(half * c + k == t)
+        def _():
+            own_copies[0].wait()
+
+    def relay(d):
+        with jax.named_scope("wo_relay"):
+            wo_relay(0, d)
+
     weight_copy(0, 0).wait()
     for i in range(per):
-        k = first_k + i
-
-        @pl.when(half * c + k == t)
-        def _():
-            own_copy.wait()
-
-        take(k)
-    with jax.named_scope("wo_relay"):
-        wo_relay(0)
+        local(near(i))
+        take(near(i))
+    relay(1)
     for i in range(per):
-        k = per - first_k + i
-
-        @pl.when(half * c + k == t)
-        def _():
-            own_copy.wait()
+        k = cross(i)
+        local(k)
 
         @pl.when(half * c + k != t)
         def _():
@@ -460,15 +485,36 @@
                 onward(k).wait_recv()
 
         take(k)
-        take_other(first_k + i)
+        if i == 0:
+            for j in range(per):
+                k = near(j)
+
+                @pl.when(half * c + k != t)
+                def _():
+                    arrival(k, 1).wait_recv()
+                    onward(k, 1).start()
+
+        take_other(near(i))
+        relay(2 + i)
+    for i in range(per):
+        k = cross(i)
+
+        @pl.when(half * c + k != t)
+        def _():
+            onward(k, 1).wait_recv()
+
+    @pl.when(home)
+    def _():
+        own_copies[1].wait()
+
     for k in range(half):
-        xs[COND * k : COND * (k + 1)] = blk_r[k, patch:piece].astype(jnp.float32)
+        xs[COND * k : COND * (k + 1)] = cnd_r[k].astype(jnp.float32)
     normed_in(None)
     for l in range(1, LAYERS):
         wo_begin(l)
     project(0, c, 0, lead)
     for i in range(per):
-        take_other(per - first_k + i)
+        take_other(cross(i))
     block_send(1 - c, None).wait_recv()
     project(0, 1 - c, 0, lead)
 
@@ -610,26 +656,20 @@
 
                 @pl.when(l == last)
                 def _():
+                    out_s[i] = new[m - patch :]
+                    depart(i)
                     if i == 0:
                         for k in range(half):
-                            out_s[k, patch:piece] = new[COND * k : COND * (k + 1)]
-                    out_s[i, 0:patch] = new[m - patch :]
-                    here = (half * c + i == t) & (goal == me)
-
-                    @pl.when(here)
-                    def _():
-                        stay(i).start()
-
-                    @pl.when(jnp.logical_not(here))
-                    def _():
-                        leave(i).start()
+                            ocn_s[k] = new[COND * k : COND * (k + 1)]
+                            depart(k, 1)
 
             if i == half - 3:
 
                 @pl.when(l < last)
                 def _():
                     with jax.named_scope("wo_relay"):
-                        wo_relay(l + 1)
+                        for d in range(1, half):
+                            wo_relay(l + 1, d)
 
         @pl.when(l < last)
         def _():
@@ -640,43 +680,22 @@
     lax.fori_loop(0, LAYERS, layer, 0)
 
     for i in range(half):
-        g, copy = enter(i)
-
-        @pl.when(home & (g != t))
-        def _():
-            copy.wait_send()
+        for j in range(2):
+            g, copy = enter(i, j)
+
+            @pl.when(home & (g != t))
+            def _():
+                copy.wait_send()
 
     for i in range(per):
-        k = first_k + i
+        k = near(i)
 
         @pl.when(half * c + k != t)
         def _():
-            onward(k).wait_send()
-
-    for s in range(2):
-        there = 2 * me + s
-        here = (group_of(there) == t) & (x * 2 + t // half == me)
-
-        @pl.when(here)
-        def _():
-            pltpu.make_async_copy(out_s.at[t % half], out_r.at[s], orr.at[s]).wait()
-
-        @pl.when(jnp.logical_not(here))
-        def _():
-            with jax.named_scope("out_wait"):
-                remote(out_s.at[0], out_r.at[s], os.at[0], orr.at[s], (t, across)).wait_recv()
-
-        out_ref[s * piece : (s + 1) * piece] = out_r[s]
-
-    for k in range(half):
-        here = (half * c + k == t) & (goal == me)
-
-        @pl.when((x == goal_x) & jnp.logical_not(here))
-        def _():
-            leave(k).wait_send()
+            for j in range(2):
+                onward(k, j).wait_send()
 
     bias_copy.wait_send()
-
     for i in range(half):
         block_send(c, i).wait_send()
     block_send(c, None).wait_send()
@@ -708,6 +727,34 @@
         return carry
 
     lax.fori_loop(0, LAYERS, drain, 0)
+
+    for k in range(half):
+        here = (half * c + k == t) & (goal == me)
+
+        @pl.when((x == goal_x) & jnp.logical_not(here))
+        def _():
+            for j in range(2):
+                leave(k, j).wait_send()
+
+    for s in range(2):
+        there = 2 * me + s
+        here = (group_of(there) == t) & (x * 2 + t // half == me)
+
+        @pl.when(here)
+        def _():
+            for j, (src, dst) in enumerate(((out_s, out_r), (ocn_s, ocn_r))):
+                pltpu.make_async_copy(src.at[t % half], dst.at[s], orr.at[j, s]).wait()
+
+        @pl.when(jnp.logical_not(here))
+        def _():
+            with jax.named_scope("out_wait"):
+                for j, (src, dst) in enumerate(((out_s, out_r), (ocn_s, ocn_r))):
+                    remote(
+                        src.at[0], dst.at[s], os.at[j, 0], orr.at[j, s], (t, across)
+                    ).wait_recv()
+
+        out_ref[s * piece : s * piece + patch] = out_r[s]
+        out_ref[s * piece + patch : (s + 1) * piece] = ocn_r[s]
 
 
 def shards_clip(
@@ -755,8 +802,10 @@
             pltpu.VMEM(fc1_weight.shape, bf16),
             pltpu.VMEM(fc2_weight.shape, bf16),
             pltpu.VMEM(fc1_bias.shape, f32),
-            pltpu.VMEM((groups, piece, D), bf16),
-            pltpu.VMEM((half, piece, D), bf16),
+            pltpu.VMEM((groups, PATCH_DEV, D), bf16),
+            pltpu.VMEM((groups, COND, D), bf16),
+            pltpu.VMEM((half, PATCH_DEV, D), bf16),
+            pltpu.VMEM((half, COND, D), bf16),
             pltpu.VMEM((rows, D), f32),
             pltpu.VMEM((rows, D), f32),
             pltpu.VMEM((LAYERS, 2, rows, D), bf16),
@@ -770,22 +819,24 @@
             pltpu.VMEM((chunk, hidden), bf16),
             pltpu.VMEM((LAYERS, rows, D), bf16),
             pltpu.VMEM((LAYERS, rows, D), bf16),
-            pltpu.VMEM((half, piece, D), bf16),
-            pltpu.VMEM((2, piece, D), bf16),
+            pltpu.VMEM((half, PATCH_DEV, D), bf16),
+            pltpu.VMEM((2, PATCH_DEV, D), bf16),
+            pltpu.VMEM((half, COND, D), bf16),
+            pltpu.VMEM((2, COND, D), bf16),
             dma((LAYERS, 4)),
-            dma((half,)),
-            dma((half,)),
-            dma((half,)),
-            dma((half,)),
-            dma((1,)),
+            dma((2, half)),
+            dma((2, half)),
+            dma((2, half)),
+            dma((2, half)),
+            dma((2,)),
             dma((1,)),
             dma((1,)),
             dma((LAYERS, 5 * (half + 1))),
             dma((LAYERS, 5 * (half + 1))),
             dma((LAYERS, SPREAD + 2 * half)),
             dma((LAYERS, SPREAD + 2 * half)),
-            dma((half,)),
-            dma((2,)),
+            dma((2, half)),
+            dma((2, 2)),
         ],
         compiler_params=pltpu.CompilerParams(
             collective_id=0, has_side_effects=True, vmem_limit_bytes=60 * 1024 * 1024

time: 82.7 us -> 79.7 us (0.964); the launches traced: 81.7 us -> 79.6 us
  Pallas kernels: 80 us -> 77.9 us
    pallas_call x1, Pallas kernels: 80 us -> 77.9 us  [shards_clip(): pl.pallas_call(clip_kernel, out_shape=jax.ShapeDtypeStruct((2 * piece, D)...]
where the time goes in v3:
time: 79.7 us; the launch traced here: 79.6 us
  Pallas kernels  77.9 us (98%)
  local copies, waits for them, and re-layouts  1.68 us (2%)
    pallas_call x1, Pallas kernels, shards_clip(): pl.pallas_call(clip_kernel, out_shape=jax.ShapeDtypeStruct((2 * piece, D)...  77.9 us
    unnamed x1, local copies, waits for them, and re-layouts  1.68 us

profile of v3, /device:TPU:0, one launch (start us, length us, event | category | flops | bytes accessed | tf_op | source)
XLA Modules:
  0.0 79.6 jit_solution(504655274551268188)
XLA Ops:
  0.0 77.9 %shard_map.145 = bf16[132,1024]{1,0:T(8,128)(2,1)} custom-call(bf16[528,1024]{1,0:T(8,128)(2,1)} %bitcast.4, s32[8]{0:T(128)} %time_ref.1, s32[8]{0:T(128)} %cond_ref.1, f32[2,1024]{1,0:T(2,128)} %g1.1, f32[2,1024]{1,0:T(2,128)} %b1.1, f32[3,2,256]{2,1,0:T(2,128)} %bitcast.5, f32[2,1024]{1,0:T(2,128)} %ob.1, f32[2,1024]{1,0:T(2,128)} %g2.1, f32[2,1024]{1,0:T(2,128)} %b2.1, ...), custom_call_target="tpu_custom_call" | custom-call | tf_op jit(solution)/shard_map/pallas_call | solution.py:792
  77.9 1.7 %copy.17 = bf16[1,132,1024]{2,1,0:T(8,128)(2,1)} copy(bf16[1,132,1024]{2,1,0:T(8,128)(2,1)} %bitcast.3) | data formatting | bytes 540672

commit v4 on v3

--- a/solution.py
+++ b/solution.py
@@ -161,8 +161,8 @@
 
 
 def clip_kernel(
-    x_ref, time_ref, cond_ref, g1, b1, qkvb, ob, g2, b2, f1b, f2b, wqkv_h, wo_h, w1_h, w2_h,
-    out_ref, wqkv, wo, w1, w2, w1p, w2p, f1p, blk_s, cnd_s, blk_r, cnd_r, xs, keep, nrm1, nrm2, qb, kb, vb, mask,
+    x_h, time_h, cond_h, g1_h, b1_h, qkvb_h, ob_h, g2_h, b2_h, f1b_h, f2b_h, wqkv_h, wo_h, w1_h,
+    w2_h, out_ref, x_ref, time_ref, cond_ref, g1, b1, qkvb, ob, g2, b2, f1b, f2b, small, wqkv, wo, w1, w2, w1p, w2p, f1p, blk_s, cnd_s, blk_r, cnd_r, xs, keep, nrm1, nrm2, qb, kb, vb, mask,
     att, att_p, inner, us, ur, out_s, out_r, ocn_s, ocn_r,
     wsem, in_s, in_r, fw_s, fw_r, loc, bs, br, ls, lr, ws, wr, os, orr,
 ):
@@ -174,9 +174,9 @@
     lead = rows - half * patch
     chunks = [(lead + i * patch, patch) for i in range(half)]
     chunks[0] = (0, lead + patch)
-    cut = lead + (half // 2) * patch
-    spans = ((0, cut), (cut, rows - cut))
     per = half // 2
+    members = [[i] for i in range(per)] + [list(range(per, half))]
+    spans = [(chunks[g[0]][0], sum(chunks[i][1] for i in g)) for g in members]
     head_dim = D // HEADS
     width = qb.shape[1]
     head_local = width // head_dim
@@ -187,6 +187,7 @@
     me = lax.axis_index("tensor")
     x = me // 2
     c = me % 2
+    mine = (c + t // half) % 2
     partner = me + 1 - 2 * c
     beside = t + 1 - 2 * (t % 2)
     across = (me + 2) % 4
@@ -211,9 +212,17 @@
             dst = wo.at[l, pl.ds(pl.multiple_of(me * width, width), width)]
         return pltpu.make_async_copy(pairs[j][0].at[l], dst, wsem.at[l, j])
 
-    for l in range(LAYERS):
-        for j in ((1, 0, 2, 3) if l == 0 else (0, 1, 2, 3)):
-            weight_copy(l, j).start()
+    fetches = [
+        pltpu.make_async_copy(src, dst, small.at[j])
+        for j, (src, dst) in enumerate(
+            (
+                (x_h, x_ref), (time_h, time_ref), (cond_h, cond_ref), (g1_h, g1), (b1_h, b1),
+                (qkvb_h, qkvb), (ob_h, ob), (g2_h, g2), (b2_h, b2), (f1b_h, f1b), (f2b_h, f2b),
+            )
+        )
+    ]
+    for copy in fetches:
+        copy.start()
 
     def remote(src, dst, s, r, to):
         return pltpu.make_async_remote_copy(
@@ -231,17 +240,21 @@
         hello((t + d) % groups, me)
     for s in range(2):
         g = group_of(2 * me + s)
-        j = x * 2 + t // half
+        j = x * 2 + (t // half + g // half) % 2
 
         @pl.when(jnp.logical_or(g != t, j != me))
         def _():
             hello(g, j)
 
+    for l in range(LAYERS):
+        for j in ((1, 0, 2, 3) if l == 0 else (0, 1, 2, 3)):
+            weight_copy(l, j).start()
+    fetches[0].wait()
     for g in range(groups):
         blk_s[g] = x_ref[g * piece : g * piece + patch]
         cnd_s[g] = x_ref[g * piece + patch : (g + 1) * piece]
 
-    home = c == t // half
+    home = c == 0
     own_copies = [
         pltpu.make_async_copy(src.at[clip], dst.at[t % half], loc.at[j])
         for j, (src, dst) in enumerate(((blk_s, blk_r), (cnd_s, cnd_r)))
@@ -259,14 +272,12 @@
         for f in range(groups):
             base = (f // half) * rows
             lo = base + lead + (f % half) * patch
-            out = jnp.where((at >= lo) & (at < lo + patch), time_ref[f], out)
+            out = jnp.where((at >= lo) & (at < lo + patch), time_ref[:, f : f + 1], out)
             lo = base + COND * (f % half)
-            hi = lo + (COND if query else cond_ref[f])
-            out = jnp.where((at >= lo) & (at < hi), time_ref[f], out)
+            hi = lo + (COND if query else cond_ref[:, f : f + 1])
+            out = jnp.where((at >= lo) & (at < hi), time_ref[:, f : f + 1], out)
         return out
 
-    mask[...] = jnp.where(times(1, False) <= times(0, True), 0.0, -1e30)
-    xs[0:lead] = jnp.zeros((lead, D), jnp.float32)
 
     targets = jnp.where(x == goal_x, half, 0)
     targets = targets - jnp.where((x == goal_x) & (goal == me) & home, 1, 0)
@@ -274,18 +285,17 @@
         pl.semaphore_wait(barrier, 3 + groups - 1 + targets)
 
     def enter(i, j):
-        far = jnp.where(x == 0, t // 2 + 2, half - 1 - t // 2)
-        z = (far + 2 * (i // 2)) % half
+        z = per * mine + (t // 2 + x) % 2
         g = 2 * z + (i + t) % 2
         k = t % half
         src, dst = ((blk_s, blk_r), (cnd_s, cnd_r))[j]
         return g, remote(src.at[clip_of(g)], dst.at[k], in_s.at[j, i], in_r.at[j, k], (g, me))
 
     for j in range(2):
-        for i in range(half):
+        for i in range(2):
             g, copy = enter(i, j)
 
-            @pl.when(home & (g != t))
+            @pl.when(g != t)
             def _():
                 copy.start()
 
@@ -344,12 +354,17 @@
             wo_row(l, d, (beside - 2 * d + groups) % groups).wait_recv()
         wo_rest(l).start()
 
+    for copy in fetches[1:]:
+        copy.wait()
     bias_copy = remote(f1b, f1p, bs.at[0], br.at[0], (t, partner))
     wo_begin(0)
     bias_copy.start()
     for copy in mlp_weights(0):
         copy.start()
 
+    mask[...] = jnp.where(times(1, False) <= times(0, True), 0.0, -1e30)
+    xs[0:lead] = jnp.zeros((lead, D), jnp.float32)
+
     def onward(k, j=0):
         at = (blk_r, cnd_r)[j].at[k]
         return remote(at, at, fw_s.at[j, k], fw_r.at[j, k], (t, across))
@@ -359,9 +374,6 @@
         return remote(src.at[0], dst.at[k], in_s.at[j, 0], in_r.at[j, k], (t, across))
 
     first_k = per * ((t // 2 + x) % 2)
-    with jax.named_scope("wo_first"):
-        wo_share(0)
-
     def near(i):
         return first_k + (i + t) % 2
 
@@ -371,12 +383,16 @@
     for i in range(per):
         k = near(i)
 
-        @pl.when(half * c + k != t)
+        @pl.when(half * mine + k != t)
         def _():
             with jax.named_scope("in_direct"):
                 arrival(k).wait_recv()
             onward(k).start()
 
+        if i == 0:
+            with jax.named_scope("wo_first"):
+                wo_share(0)
+
     def norm(v, gain, bias):
         return layer_norm(v, gain, bias).astype(jnp.bfloat16)
 
@@ -387,11 +403,11 @@
         return ls.at[l, kind * (half + 1) + i], lr.at[l, kind * (half + 1) + i]
 
     def normed_send(l, i):
-        at = nrm1.at[l, c, pl.ds(*chunks[i])]
+        at = nrm1.at[l, mine, pl.ds(*chunks[i])]
         return remote(at, at, *ids(l, N1, i), (t, partner))
 
     def normed_come(l, i):
-        at = nrm1.at[l, 1 - c, pl.ds(*chunks[i])]
+        at = nrm1.at[l, 1 - mine, pl.ds(*chunks[i])]
         return remote(at, at, *ids(l, N1, i), (t, partner))
 
     def att_send(l, i, kind):
@@ -412,14 +428,14 @@
     def leave(k, j=0):
         src, dst = ((out_s, out_r), (ocn_s, ocn_r))[j]
         s = clip % 2
-        return remote(src.at[k], dst.at[s], os.at[j, k], orr.at[j, s], (half * c + k, goal))
+        return remote(src.at[k], dst.at[s], os.at[j, k], orr.at[j, s], (half * mine + k, goal))
 
     def stay(k, j=0):
         src, dst = ((out_s, out_r), (ocn_s, ocn_r))[j]
         return pltpu.make_async_copy(src.at[k], dst.at[clip % 2], orr.at[j, clip % 2])
 
     def depart(k, j=0):
-        here = (half * c + k == t) & (goal == me)
+        here = (half * mine + k == t) & (goal == me)
 
         @pl.when(here)
         def _():
@@ -448,21 +464,21 @@
 
     def normed_in(i):
         at = strip(i)
-        nrm1[0, c, at] = norm(xs[at], g1[0:1], b1[0:1])
-        block_send(c, i).start()
+        nrm1[0, mine, at] = norm(xs[at], g1[0:1], b1[0:1])
+        block_send(mine, i).start()
 
     def take(k):
         xs[strip(k)] = blk_r[k].astype(jnp.float32)
         normed_in(k)
-        project(0, c, lead + k * patch, patch)
+        project(0, mine, lead + k * patch, patch)
 
     def take_other(k):
         with jax.named_scope("n1_wait"):
-            block_send(1 - c, k).wait_recv()
-        project(0, 1 - c, lead + k * patch, patch)
+            block_send(1 - mine, k).wait_recv()
+        project(0, 1 - mine, lead + k * patch, patch)
 
     def local(k):
-        @pl.when(half * c + k == t)
+        @pl.when(half * mine + k == t)
         def _():
             own_copies[0].wait()
 
@@ -479,7 +495,7 @@
         k = cross(i)
         local(k)
 
-        @pl.when(half * c + k != t)
+        @pl.when(half * mine + k != t)
         def _():
             with jax.named_scope("in_cross"):
                 onward(k).wait_recv()
@@ -489,17 +505,18 @@
             for j in range(per):
                 k = near(j)
 
-                @pl.when(half * c + k != t)
+                @pl.when(half * mine + k != t)
                 def _():
                     arrival(k, 1).wait_recv()
                     onward(k, 1).start()
 
         take_other(near(i))
-        relay(2 + i)
+    for d in range(2, half):
+        relay(d)
     for i in range(per):
         k = cross(i)
 
-        @pl.when(half * c + k != t)
+        @pl.when(half * mine + k != t)
         def _():
             onward(k, 1).wait_recv()
 
@@ -512,11 +529,11 @@
     normed_in(None)
     for l in range(1, LAYERS):
         wo_begin(l)
-    project(0, c, 0, lead)
+    project(0, mine, 0, lead)
     for i in range(per):
         take_other(cross(i))
-    block_send(1 - c, None).wait_recv()
-    project(0, 1 - c, 0, lead)
+    block_send(1 - mine, None).wait_recv()
+    project(0, 1 - mine, 0, lead)
 
     lane = lax.broadcasted_iota(jnp.int32, (1, width), 1)
     heads = [(lane >= h * head_dim) & (lane < (h + 1) * head_dim) for h in range(head_local)]
@@ -547,13 +564,13 @@
 
         for i, (r0, m) in enumerate(spans):
             with jax.named_scope("attend_other"):
-                att_p[l, r0 : r0 + m] = attend(1 - c, r0, m)
+                att_p[l, r0 : r0 + m] = attend(1 - mine, r0, m)
             att_send(l, i, AD).start()
             att_send(l, i, AP).start()
             with jax.named_scope("attend_own"):
-                att[l, me, r0 : r0 + m] = attend(c, r0, m)
+                att[l, me, r0 : r0 + m] = attend(mine, r0, m)
             att_send(l, i, AO).start()
-            if i == 0:
+            if i == per - 1:
                 with jax.named_scope("wo_finish"):
                     wo_finish(l)
 
@@ -615,7 +632,7 @@
 
             @pl.when(sends_x)
             def _():
-                for j in range(per * i, per * (i + 1)):
+                for j in members[i]:
                     cross_send(l, j).start()
 
             if i == 0:
@@ -631,7 +648,7 @@
         def other(i):
             with jax.named_scope("n1_wait"):
                 normed_come(l + 1, i).wait_recv()
-            project(l + 1, 1 - c, *chunks[i])
+            project(l + 1, 1 - mine, *chunks[i])
 
         for i, (r0, m) in enumerate(chunks):
 
@@ -646,11 +663,11 @@
                 def _():
                     wide = new.astype(jnp.float32)
                     xs[r0 : r0 + m] = wide
-                    nrm1[l + 1, c, r0 : r0 + m] = norm(
+                    nrm1[l + 1, mine, r0 : r0 + m] = norm(
                         wide, g1[pl.ds(l + 1, 1)], b1[pl.ds(l + 1, 1)]
                     )
                     normed_send(l + 1, i).start()
-                    project(l + 1, c, r0, m)
+                    project(l + 1, mine, r0, m)
                     if i > 0:
                         other(i - 1)
 
@@ -679,26 +696,26 @@
 
     lax.fori_loop(0, LAYERS, layer, 0)
 
-    for i in range(half):
+    for i in range(2):
         for j in range(2):
             g, copy = enter(i, j)
 
-            @pl.when(home & (g != t))
+            @pl.when(g != t)
             def _():
                 copy.wait_send()
 
     for i in range(per):
         k = near(i)
 
-        @pl.when(half * c + k != t)
+        @pl.when(half * mine + k != t)
         def _():
             for j in range(2):
                 onward(k, j).wait_send()
 
     bias_copy.wait_send()
     for i in range(half):
-        block_send(c, i).wait_send()
-    block_send(c, None).wait_send()
+        block_send(mine, i).wait_send()
+    block_send(mine, None).wait_send()
 
     def drain(l, carry):
         for i in range(half):
@@ -728,17 +745,9 @@
 
     lax.fori_loop(0, LAYERS, drain, 0)
 
-    for k in range(half):
-        here = (half * c + k == t) & (goal == me)
-
-        @pl.when((x == goal_x) & jnp.logical_not(here))
-        def _():
-            for j in range(2):
-                leave(k, j).wait_send()
-
     for s in range(2):
         there = 2 * me + s
-        here = (group_of(there) == t) & (x * 2 + t // half == me)
+        here = (group_of(there) == t) & home
 
         @pl.when(here)
         def _():
@@ -755,6 +764,14 @@
 
         out_ref[s * piece : s * piece + patch] = out_r[s]
         out_ref[s * piece + patch : (s + 1) * piece] = ocn_r[s]
+
+    for k in range(half):
+        here = (half * mine + k == t) & (goal == me)
+
+        @pl.when((x == goal_x) & jnp.logical_not(here))
+        def _():
+            for j in range(2):
+                leave(k, j).wait_send()
 
 
 def shards_clip(
@@ -782,19 +799,30 @@
     hidden = fc1_weight.shape[2]
     lead = -(-half * COND // 16) * 16
     rows = lead + half * PATCH_DEV
-    chunk = lead + (half // 2) * PATCH_DEV
+    chunk = lead + (half - half // 2) * PATCH_DEV
 
     vmem = pl.BlockSpec(memory_space=pltpu.VMEM)
-    smem = pl.BlockSpec(memory_space=pltpu.SMEM)
     hbm = pl.BlockSpec(memory_space=pl.ANY)
     bf16, f32 = jnp.bfloat16, jnp.float32
     dma = pltpu.SemaphoreType.DMA
     out = pl.pallas_call(
         clip_kernel,
         out_shape=jax.ShapeDtypeStruct((2 * piece, D), bf16),
-        in_specs=[vmem, smem, smem] + [vmem] * 8 + [hbm] * 4,
+        in_specs=[hbm] * 15,
         out_specs=vmem,
         scratch_shapes=[
+            pltpu.VMEM(frames_in.shape[1:], bf16),
+            pltpu.VMEM((1, groups), jnp.int32),
+            pltpu.VMEM((1, groups), jnp.int32),
+            pltpu.VMEM(ln1_gain.shape, f32),
+            pltpu.VMEM(ln1_bias.shape, f32),
+            pltpu.VMEM((3, LAYERS, width), f32),
+            pltpu.VMEM(out_bias.shape, f32),
+            pltpu.VMEM(ln2_gain.shape, f32),
+            pltpu.VMEM(ln2_bias.shape, f32),
+            pltpu.VMEM(fc1_bias.shape, f32),
+            pltpu.VMEM(fc2_bias.shape, f32),
+            dma((11,)),
             pltpu.VMEM(qkv_weight.shape, bf16),
             pltpu.VMEM((LAYERS, D, D), bf16),
             pltpu.VMEM(fc1_weight.shape, bf16),
@@ -843,8 +871,8 @@
         ),
     )(
         frames_in[0],
-        frame_time,
-        cond_count,
+        frame_time.reshape(1, groups),
+        cond_count.reshape(1, groups),
         ln1_gain,
         ln1_bias,
         qkv_bias.transpose(1, 0, 2),

time: 79.7 us -> 76.8 us (0.964)
  Pallas kernels: 77.9 us -> 74.9 us
    pallas_call x1, Pallas kernels: 77.9 us -> 74.9 us  [shards_clip(): pl.pallas_call(clip_kernel, out_shape=jax.ShapeDtypeStruct((2 * piece, D)...]
where the time goes in v4:
time: 76.8 us; the launch traced here: 76.6 us
  Pallas kernels  74.9 us (98%)
  local copies, waits for them, and re-layouts  1.68 us (2%)
    pallas_call x1, Pallas kernels, shards_clip(): pl.pallas_call(clip_kernel, out_shape=jax.ShapeDtypeStruct((2 * piece, D)...  74.9 us
    unnamed x1, local copies, waits for them, and re-layouts  1.68 us

profile of v4, /device:TPU:0, one launch (start us, length us, event | category | flops | bytes accessed | tf_op | source)
XLA Modules:
  0.0 76.6 jit_solution(4260492010455267791)
XLA Ops:
  0.0 74.9 %shard_map.145 = bf16[132,1024]{1,0:T(8,128)(2,1)} custom-call(bf16[528,1024]{1,0:T(8,128)(2,1)} %bitcast.6, s32[1,8]{1,0:T(1,128)} %bitcast.8, s32[1,8]{1,0:T(1,128)} %bitcast.9, f32[2,1024]{1,0:T(2,128)} %g1_h.1, f32[2,1024]{1,0:T(2,128)} %b1_h.1, f32[3,2,256]{2,1,0:T(2,128)} %bitcast.7, f32[2,1024]{1,0:T(2,128)} %ob_h.1, f32[2,1024]{1,0:T(2,128)} %g2_h.1, ...), custom_call_target="tpu_custom_call" | custom-call | tf_op jit(solution)/shard_map/pallas_call | solution.py:808
  74.9 1.7 %copy.17 = bf16[1,132,1024]{2,1,0:T(8,128)(2,1)} copy(bf16[1,132,1024]{2,1,0:T(8,128)(2,1)} %bitcast.5) | data formatting | bytes 540672
